TPU v7x, 32 devices: a whole 2x2x4 slice. The times are simulated.
32 devices in a mesh: band: 8 (over z, y), grid: 4 (over x, core).
Axes of the slice: x: 2, y: 2, z: 4, core: 2. Of those that a mesh axis runs over, the one named last changes fastest.
Arguments:
- bands: bfloat16 [2, 16, 128, 128, 128], P(None, 'band', 'grid'), may hold values from -6 to 6
- occupations: float32 [16], P('band'), may hold values from 0.25 to 1
- external: float32 [128, 128, 128], P('grid'), may hold values from 0 to 2
- density_in: float32 [128, 128, 128], P('grid'), may hold values from -0.2 to 1.4
- prev_density: float32 [128, 128, 128], P('grid'), may hold values from 0 to 1.2
- prev_residual: float32 [128, 128, 128], P('grid'), may hold values from -1.3 to 0.3
- hist_density: float32 [5, 128, 128, 128], P(None, 'grid'), may hold values from 0 to 1
- hist_residual: float32 [5, 128, 128, 128], P(None, 'grid'), may hold values from -0.6 to 1
Outputs:
- density: float32 [128, 128, 128], P('grid')
- residual: float32 [128, 128, 128], P('grid')
All inputs are finite; a program needn't handle non-finite values.
Results may differ from a plain program's by a relative error of at most 0.018.
The roundings to bfloat16 on the way count: a program that leaves them out, or rounds other values in their place, can miss the bound.
Values may be sent and summed in bfloat16 or wider, within the bound.
No kernel may reach another device: no remote copies, remote signals or barrier semaphores. Data moves between devices by JAX's collectives and lax.ppermute only.
A program may use at most 192 MiB of HBM per device.

v0:
```python
import functools
import math

import jax
import jax.numpy as jnp
import ml_dtypes
import numpy as np
from jax import lax
from jax.experimental import pallas as pl
from jax.experimental.pallas import tpu as pltpu
from jax.sharding import PartitionSpec as P


DEPTH = 6
ITERS = 3
LANES = 128
PLANES = 16
FILTER_STEPS = 1

time_step = 0.25
energy_shift = 2.5
mixing_weight = 0.5
ridge_share = 0.1
ridge_floor = 0.01
density_scale = 8.0


f32 = jnp.float32
bf16 = jnp.bfloat16


def fourier_tables(length, groups):
    frequency = np.arange(-(length // 4), length // 4)
    phase_index = np.arange(length)[:, None] * frequency[None, :] % length
    angles = phase_index.astype(np.float32) * np.float32(2.0 * math.pi / length)
    unit_scale = np.float32(1.0 / math.sqrt(length))
    cos, sin = (f(angles).astype(np.float32) * unit_scale for f in (np.cos, np.sin))
    out = [
        np.block([[cos, -sin], [sin, cos]]),
        np.block([[cos.T, sin.T], [-sin.T, cos.T]]),
    ]
    stacks = [[], [], [], []]
    for index in range(groups):
        def ordered(count):
            return np.concatenate([np.arange(count // groups) + (index ^ m) * (count // groups) for m in range(groups)])

        ck, sk = (v[:, ordered(len(frequency))] for v in (cos, sin))
        cx, sx = (v[ordered(length)] for v in (cos, sin))
        stacks[0].append(np.concatenate([ck.T, sk.T], axis=0))
        stacks[1].append(np.concatenate([ck, sk], axis=1))
        stacks[2].append(np.concatenate([cx.T, sx.T], axis=0))
        stacks[3].append(np.concatenate([cx, sx], axis=1))
    return [jnp.asarray(v.astype(ml_dtypes.bfloat16)) for v in out + [np.stack(v) for v in stacks]]


def dot(a, b):
    return jnp.dot(a, b, preferred_element_type=f32)


def swap_halves(v):
    return pltpu.roll(v, v.shape[-1] // 2, v.ndim - 1)


def half_sign(shape, first):
    lane = lax.broadcasted_iota(jnp.int32, shape, len(shape) - 1)
    return jnp.where(lane < shape[-1] // 2, first, -first).astype(f32)


def orders(devices):
    bits = devices.bit_length() - 1
    upper = list(range(bits))
    lower = ([1, 0] + upper[2:]) if bits > 1 else upper
    return upper, lower


def position(relative, order):
    out = None
    for i, bit in enumerate(order):
        part = lax.shift_left(lax.bitwise_and(lax.shift_right_logical(relative, bit), 1), len(order) - 1 - i)
        out = part if out is None else out + part
    return out


def units(half, devices, step, step_rows, row, count, me):
    assert step_rows % (2 * half) == 0
    unit = min(count, half)
    for at in range(0, count, unit):
        block, within = divmod(row + at, 2 * half)
        which, offset = divmod(within, half)
        relative = lax.bitwise_xor(step * (step_rows // (2 * half)) + block, me)
        yield which, position(relative, orders(devices)[which]), offset, at, unit


def read_rows(refs, step, step_rows, row, count, me):
    near, half = refs[0].shape[:2]
    out = []
    for which, at, offset, _, unit in units(half, 2 * near, step, step_rows, row, count, me):
        here = (lax.rem(at, near), pl.ds(offset, unit), slice(None))
        low, high = (refs[2 * which + i][here].astype(f32) for i in range(2))
        out.append(jnp.where(at < near, low, high))
    return out[0] if len(out) == 1 else jnp.concatenate(out, axis=0)


def write_rows(refs, step, step_rows, row, value, me):
    devices, half = refs[0].shape[:2]
    for which, to, offset, at, unit in units(half, devices, step, step_rows, row, value.shape[0], me):
        refs[which][to, pl.ds(offset, unit), :] = value[at : at + unit]


def solve_rows(gram, rhs):
    n = len(rhs)
    trace = gram[0][0]
    for j in range(1, n):
        trace = trace + gram[j][j]
    ridge = ridge_share * trace / n + ridge_floor
    a = [[gram[j][k] + ridge if j == k else gram[j][k] for k in range(n)] for j in range(n)]
    low = [[None] * n for _ in range(n)]
    diag = [None] * n
    inv = [None] * n
    for j in range(n):
        value = a[j][j]
        scaled = []
        for k in range(j):
            s = low[j][k] * diag[k]
            scaled.append(s)
            value = value - low[j][k] * s
        diag[j] = value
        inv[j] = 1.0 / value
        for r in range(j + 1, n):
            e = a[r][j]
            for k in range(j):
                e = e - low[r][k] * scaled[k]
            low[r][j] = e * inv[j]
    mid = []
    for j in range(n):
        e = rhs[j]
        for k in range(j):
            e = e - low[j][k] * mid[k]
        mid.append(e)
    out = [None] * n
    for j in reversed(range(n)):
        e = mid[j] * inv[j]
        for k in range(j + 1, n):
            e = e - low[k][j] * out[k]
        out[j] = e
    return out


def pair_index(n):
    return {(j, k): i for i, (j, k) in enumerate((j, k) for j in range(n) for k in range(j, n))}


STAT_ROWS = 32


def spread_diagonal(row):
    shape = (STAT_ROWS, LANES)
    lane = lax.broadcasted_iota(jnp.int32, shape, 1)
    own = lax.broadcasted_iota(jnp.int32, shape, 0)
    picked = jnp.where(lane == own, jnp.broadcast_to(row, shape), 0.0)
    return jnp.broadcast_to(jnp.sum(picked, axis=1, keepdims=True), shape)


def finish_stats(stats_ref, carry_ref, first, cells):
    total = spread_diagonal(stats_ref[...] * (1.0 / cells))
    n = DEPTH
    gram = [[None] * n for _ in range(n)]
    kept = pair_index(n - 1)
    for (j, k), i in kept.items():
        value = total[2 * n + i : 2 * n + i + 1] if first else carry_ref[i : i + 1, :]
        gram[j][k] = value
        gram[k][j] = value
    for j in range(n):
        value = total[j : j + 1]
        gram[j][n - 1] = value
        gram[n - 1][j] = value
    rhs = [total[n + j : n + j + 1] for j in range(n)]
    return gram, rhs


CARRY_ROWS = 16


def combine_kernel(tie_ref, r_ref, q_ref, s_ref):
    s_ref[...] = (r_ref[...] + mixing_weight * q_ref[...]).astype(s_ref.dtype)


def combine(tie, hist_density, hist_residual, j, parts):
    _, rows, lanes = hist_density.shape
    block = rows // parts
    spec = pl.BlockSpec((None, block, lanes), lambda s, t: (j, s, 0))
    return pl.pallas_call(
        combine_kernel,
        grid_spec=pltpu.PrefetchScalarGridSpec(
            num_scalar_prefetch=1,
            grid=(parts,),
            in_specs=[spec, spec],
            out_specs=pl.BlockSpec((block, lanes), lambda s, t: (s, 0)),
        ),
        out_shape=jax.ShapeDtypeStruct((rows, lanes), bf16),
        compiler_params=pltpu.CompilerParams(vmem_limit_bytes=12 << 20),
        cost_estimate=pl.CostEstimate(flops=10**8, bytes_accessed=rows * lanes * 10, transcendentals=0),
        name="combine",
    )(tie, hist_density, hist_residual)


def middle_kernel(me_ref, *refs):
    rho_refs, (in_ref, prev_ref, mid_ref, new_ref) = refs[:4], refs[4:]
    rows = in_ref.shape[0]
    for base in range(0, rows, LANES):
        here = pl.ds(base, LANES)
        rho_out = read_rows(rho_refs, pl.program_id(0), rows, base, LANES, me_ref[0])
        mid = mixing_weight * (rho_out + in_ref[here, :])
        mid_ref[here, :] = mid
        new_ref[here, :] = (mid - prev_ref[here, :]).astype(new_ref.dtype)


def middle(me, slab, rho, rho_in, prev_mid):
    planes = min(PLANES, slab)
    rows, block = rho_in.shape[0], planes * LANES
    spec = pl.BlockSpec((block, LANES), lambda s, m: (s, 0))
    const = lambda shape: pl.BlockSpec(shape, lambda s, m: (0,) * len(shape))
    return pl.pallas_call(
        middle_kernel,
        grid_spec=pltpu.PrefetchScalarGridSpec(
            num_scalar_prefetch=1,
            grid=(rows // block,),
            in_specs=[const(v.shape) for v in rho] + [spec, spec],
            out_specs=[spec, spec],
        ),
        out_shape=[jax.ShapeDtypeStruct((rows, LANES), f32), jax.ShapeDtypeStruct((rows, LANES), bf16)],
        compiler_params=pltpu.CompilerParams(vmem_limit_bytes=12 << 20),
        cost_estimate=pl.CostEstimate(flops=10**8, bytes_accessed=rows * LANES * 12, transcendentals=0),
        name="middle",
    )(me, *rho, rho_in, prev_mid)


def row_sum(v):
    return jnp.sum(v, axis=0, keepdims=True)


def finish_kernel(mine_ref, got_ref, upper_ref, lower_ref):
    for i in range(4):
        v = (mine_ref[i].astype(f32) + got_ref[i ^ 1].astype(f32)).astype(bf16)
        (upper_ref, lower_ref)[i // 2][i % 2] = v


def finish(mine, got):
    return pl.pallas_call(
        finish_kernel,
        out_shape=[jax.ShapeDtypeStruct((2,) + mine.shape[1:], bf16)] * 2,
        compiler_params=pltpu.CompilerParams(vmem_limit_bytes=8 << 20),
        cost_estimate=pl.CostEstimate(flops=10**6, bytes_accessed=3 * mine.size, transcendentals=0),
        name="finish",
    )(mine, got)


def dots_kernel(first, at_ref, *refs):
    q_count = DEPTH - 1
    upper_ref, lower_ref, own_in, far_in, prev_ref, hist_ref = refs[:6]
    recent, (stats_ref, newest_ref, res_ref) = refs[6:-3], refs[-3:]
    half = upper_ref.shape[1]
    total = None
    for side, in_ref in enumerate((own_in, far_in)):
        rows = []
        for part in range(2):
            here = slice(part * half, (part + 1) * half)
            q = [hist_ref[j, side, here, :] for j in range(len(recent), q_count)] + [r[side, here, :] for r in recent]
            res = (upper_ref, lower_ref)[part][side].astype(f32) - in_ref[here, :]
            newest = res - prev_ref[side, here, :]
            newest_ref[side, here, :] = newest
            res_ref[side, here, :] = res
            out = [row_sum(v * newest) for v in q] + [row_sum(newest * newest)]
            out += [row_sum(v * res) for v in q] + [row_sum(newest * res)]
            if first:
                for j, k in pair_index(q_count):
                    out.append(row_sum(q[j] * q[k]))
            out += [jnp.zeros((1, LANES), f32)] * (STAT_ROWS - len(out))
            rows.append(jnp.concatenate(out, axis=0))
        table = rows[0] + rows[1]
        total = table if total is None else total + table
    table = jnp.sum(total, axis=1, keepdims=True)
    shape = (STAT_ROWS, LANES)
    lane = lax.broadcasted_iota(jnp.int32, shape, 1)
    own = lax.broadcasted_iota(jnp.int32, shape, 0)
    stats_ref[...] = row_sum(jnp.where(lane == own, jnp.broadcast_to(table, shape), 0.0))


def dots(first, at, upper, lower, rho_in, prev_res, hist, recent):
    half = upper.shape[1]
    block = 2 * half
    const = lambda shape: pl.BlockSpec(shape, lambda s, m: (0,) * len(shape))
    pair = (2, block, LANES)
    return pl.pallas_call(
        functools.partial(dots_kernel, first),
        grid_spec=pltpu.PrefetchScalarGridSpec(
            num_scalar_prefetch=1,
            grid=(1,),
            in_specs=[
                const(upper.shape),
                const(lower.shape),
                pl.BlockSpec((block, LANES), lambda s, m: (m[0], 0)),
                pl.BlockSpec((block, LANES), lambda s, m: (m[1], 0)),
                const(pair),
                const(hist.shape),
            ]
            + [const(pair)] * len(recent),
            out_specs=[const((1, LANES)), const(pair), const(pair)],
        ),
        out_shape=[
            jax.ShapeDtypeStruct((1, LANES), f32),
            jax.ShapeDtypeStruct(pair, f32),
            jax.ShapeDtypeStruct(pair, f32),
        ],
        compiler_params=pltpu.CompilerParams(vmem_limit_bytes=14 << 20),
        cost_estimate=pl.CostEstimate(flops=1, bytes_accessed=block * LANES * 64, transcendentals=0),
        name="dots",
    )(at, upper, lower, rho_in, rho_in, prev_res, hist, *recent)


def mix_plane(me, coeffs, step, step_rows, base, rows, rho_refs, in_ref, prev_mid_ref, s_refs):
    rho_out = read_rows(rho_refs, step, step_rows, base, rows, me)
    here = pl.ds(base, rows)
    rho_in = in_ref[here, :]
    mid = mixing_weight * (rho_out + rho_in)
    dens = mid - coeffs[-1] * (mid - prev_mid_ref[here, :])
    for c, ref in zip(coeffs, s_refs):
        dens = dens - c * ref[here, :].astype(f32)
    return dens, rho_out - rho_in


def forward_kernel(kind, planes, first, groups, cells, me_ref, *refs):
    refs = list(refs)
    take = lambda k: [refs.pop(0) for _ in range(k)]
    mixing = kind != "plain"
    me = me_ref[0]
    if mixing:
        (stats_ref,) = take(1)
        carry_ref = None if first else take(1)[0]
        rho_refs = take(4)
        in_ref, prev_mid_ref = take(2)
        s_refs = take(DEPTH - 1)
    else:
        (in_ref,) = take(1)
    if kind != "last":
        ext_ref, psi_ref, wz_ref, ly_ref = take(4)
        out_refs = take(groups)
    if mixing:
        dens_ref, second = take(2)
        (coeff_ref,) = take(1)

        @pl.when(pl.program_id(0) == 0)
        def _():
            gram, rhs = finish_stats(stats_ref, carry_ref, first, cells)
            for j, c in enumerate(solve_rows(gram, rhs)):
                coeff_ref[j : j + 1, :] = c
            if kind == "mix":
                second[...] = jnp.zeros_like(second)
                for (j, k), i in pair_index(DEPTH - 1).items():
                    second[i : i + 1, :] = gram[j + 1][k + 1]

        coeffs = [coeff_ref[j : j + 1, :] for j in range(DEPTH)]
    if kind != "last":
        w_ref, a_ref, scratch = take(3)
    for xi in range(planes):
        here = pl.ds(xi * LANES, LANES)
        if mixing:
            dens, res = mix_plane(
                me, coeffs, pl.program_id(0), planes * LANES, xi * LANES, LANES,
                rho_refs, in_ref, prev_mid_ref, s_refs,
            )
            dens_ref[here, :] = dens
            if kind == "last":
                second[here, :] = res
        else:
            dens = in_ref[here, :]
        if kind != "last":
            factor = jnp.exp(-time_step * (ext_ref[here, :] + dens - energy_shift))
            for c in range(2):
                w_ref[here, c * LANES : (c + 1) * LANES] = (psi_ref[c, xi].astype(f32) * factor).astype(bf16)
    if kind == "last":
        return
    kept = ly_ref.shape[0] // 2
    sign = half_sign((kept, LANES), 1.0)
    a_ref[...] = dot(w_ref[...], wz_ref[...]).astype(bf16)
    for pair in pairs(planes):
        wide = [a_ref[xi * LANES : (xi + 1) * LANES, :] for xi in pair]
        t = dot(ly_ref[...], jnp.concatenate(wide, axis=1))
        for i, xi in enumerate(pair):
            lanes = slice(i * LANES, (i + 1) * LANES)
            out = t[:kept, lanes] + sign * swap_halves(t[kept:, lanes])
            scratch[pl.ds(xi, kept, stride=planes), :] = out
    per = kept // groups
    for g in range(groups):
        rows = scratch[g * per * planes : (g + 1) * per * planes, :]
        out_refs[g][...] = rows.reshape(per, planes, LANES).astype(bf16)


def table_spec(table):
    return pl.BlockSpec((None,) + table.shape[1:], lambda s, m: (m[1], 0, 0))


def pairs(count):
    return [tuple(range(i, min(i + 2, count))) for i in range(0, count, 2)]


def forward(kind, me, slab, groups, cells, ext=None, psi=None, band=0, wz=None, ly=None, density=None, mix=None):
    planes = min(PLANES, slab)
    steps = slab // planes
    block = planes * LANES
    rows = slab * LANES
    const = lambda shape: pl.BlockSpec(shape, lambda s, m: (0,) * len(shape))
    rowspec = pl.BlockSpec((block, LANES), lambda s, m: (s, 0))
    args, specs, outs, out_specs, scratch = [], [], [], [], []
    first = False
    if kind != "plain":
        first = mix["carry"] is None
        small = [mix["stats"]] + ([] if first else [mix["carry"]]) + list(mix["rho"])
        args += small
        specs += [const(v.shape) for v in small]
        wide = [mix["rho_in"], mix["prev_mid"]] + list(mix["orig"]) + list(mix["extra"])
        args += wide
        specs += [rowspec] * len(wide)
    else:
        args.append(density)
        specs.append(rowspec)
    if kind != "last":
        kept = ly.shape[1] // 2
        per = kept // groups
        args += [ext, psi, wz, ly]
        specs += [
            rowspec,
            pl.BlockSpec((2, None, planes, LANES, LANES), lambda s, m: (0, band, s, 0, 0)),
            const(wz.shape),
            table_spec(ly),
        ]
        outs += [jax.ShapeDtypeStruct((per, slab, LANES), bf16)] * groups
        out_specs += [pl.BlockSpec((per, planes, LANES), lambda s, m: (0, s, 0))] * groups
    if kind != "plain":
        outs.append(jax.ShapeDtypeStruct((rows, LANES), f32))
        out_specs.append(rowspec)
        if kind == "mix":
            outs.append(jax.ShapeDtypeStruct((CARRY_ROWS, LANES), f32))
            out_specs.append(const((CARRY_ROWS, LANES)))
        else:
            outs.append(jax.ShapeDtypeStruct((rows, LANES), f32))
            out_specs.append(rowspec)
        scratch.append(pltpu.VMEM((8, LANES), f32))
    if kind != "last":
        scratch += [
            pltpu.VMEM((block, 2 * LANES), bf16),
            pltpu.VMEM((block, LANES), bf16),
            pltpu.VMEM((kept * planes, LANES), f32),
        ]
    return pl.pallas_call(
        functools.partial(forward_kernel, kind, planes, first, groups, cells),
        grid_spec=pltpu.PrefetchScalarGridSpec(
            num_scalar_prefetch=1, grid=(steps,), in_specs=specs, out_specs=out_specs, scratch_shapes=scratch
        ),
        out_shape=outs,
        compiler_params=pltpu.CompilerParams(vmem_limit_bytes=20 << 20),
        cost_estimate=pl.CostEstimate(flops=10**9, bytes_accessed=6 << 20, transcendentals=0),
    )(me, *args)


def filter_kernel(groups, me_ref, *refs):
    in_refs, refs = refs[:groups], refs[groups:]
    lf_ref, li_ref, kin_ref = refs[:3]
    out_refs = refs[3:]
    per, slab, _ = in_refs[0].shape
    kept = lf_ref.shape[0] // 2
    fsign = half_sign((kept, LANES), 1.0)
    isign = half_sign((kept, LANES), -1.0)
    for pair in pairs(per):
        wide = [jnp.concatenate([r[k] for r in in_refs], axis=0) for k in pair]
        t = dot(lf_ref[...], jnp.concatenate(wide, axis=1))
        both = []
        for i, k in enumerate(pair):
            lanes = slice(i * LANES, (i + 1) * LANES)
            c = (t[:kept, lanes] + fsign * swap_halves(t[kept:, lanes])) * kin_ref[k]
            both.append(jnp.concatenate([c.astype(bf16), (isign * swap_halves(c)).astype(bf16)], axis=0))
        d = dot(li_ref[...], jnp.concatenate(both, axis=1)).astype(bf16)
        for i, k in enumerate(pair):
            for g in range(groups):
                out_refs[g][k] = d[g * slab : (g + 1) * slab, i * LANES : (i + 1) * LANES]


def x_filter(me, blocks, lf, li, kinetic):
    groups = len(blocks)
    per, slab, _ = blocks[0].shape
    split = FILTER_STEPS if per % (2 * FILTER_STEPS) == 0 else 1
    spec = pl.BlockSpec((per // split, slab, LANES), lambda s, m: (s, 0, 0))
    return pl.pallas_call(
        functools.partial(filter_kernel, groups),
        grid_spec=pltpu.PrefetchScalarGridSpec(
            num_scalar_prefetch=1,
            grid=(split,),
            in_specs=[spec] * groups
            + [
                table_spec(lf),
                table_spec(li),
                pl.BlockSpec((per // split,) + kinetic.shape[1:], lambda s, m: (s, 0, 0)),
            ],
            out_specs=[spec] * groups,
        ),
        out_shape=[jax.ShapeDtypeStruct(blocks[0].shape, bf16)] * groups,
        compiler_params=pltpu.CompilerParams(vmem_limit_bytes=12 << 20),
        cost_estimate=pl.CostEstimate(flops=5 * 10**8, bytes_accessed=2 << 20, transcendentals=0),
        name="x_filter",
    )(me, *blocks, lf, li, kinetic)


def inverse_kernel(groups, planes, scale, band, adds, ends, keep_psi, me_ref, *refs):
    in_refs, refs = refs[:groups], refs[groups:]
    occ_ref, liy_ref, wiz_ref = refs[:3]
    refs = list(refs[3:])
    if adds:
        part_ref = refs.pop(0)
    if keep_psi:
        psi_ref = refs.pop(0)
    if ends:
        rho_refs = [refs.pop(0) for _ in range(2)]
    else:
        total_ref = refs.pop(0)
    scratch, e_ref = refs
    me = me_ref[0]
    per = in_refs[0].shape[0]
    kept = per * groups
    isign = half_sign((kept, LANES), -1.0)
    for g in range(groups):
        scratch[g * per * planes : (g + 1) * per * planes, :] = (
            in_refs[g][...].astype(f32).reshape(per * planes, LANES)
        )
    for pair in pairs(planes):
        both = []
        for xi in pair:
            v = scratch[pl.ds(xi, kept, stride=planes), :]
            both.append(jnp.concatenate([v.astype(bf16), (isign * swap_halves(v)).astype(bf16)], axis=0))
        e = dot(liy_ref[...], jnp.concatenate(both, axis=1)).astype(bf16)
        for i, xi in enumerate(pair):
            e_ref[xi * LANES : (xi + 1) * LANES, :] = e[:, i * LANES : (i + 1) * LANES]
    for xi in range(planes):
        here = pl.ds(xi * LANES, LANES)
        psi = dot(e_ref[here, :], wiz_ref[...]).astype(bf16)
        re, im = psi[:, :LANES], psi[:, LANES:]
        if keep_psi:
            psi_ref[0, xi] = re
            psi_ref[1, xi] = im
        re, im = re.astype(f32), im.astype(f32)
        total = (occ_ref[band] * scale) * (re * re + im * im)
        if adds:
            total = total + part_ref[here, :]
        if ends:
            write_rows(rho_refs, pl.program_id(0), planes * LANES, xi * LANES, total.astype(bf16), me)
        else:
            total_ref[here, :] = total


def inverse(me, blocks, occ, band, bands, liy, wiz, band_devices, scale, keep_psi, part):
    groups = len(blocks)
    per, slab, _ = blocks[0].shape
    planes = min(PLANES, slab)
    rows, block = slab * LANES, planes * LANES
    half = rows // band_devices // 2
    adds, ends = part is not None, band == bands - 1
    spec = pl.BlockSpec((per, planes, LANES), lambda s, m: (0, s, 0))
    rowspec = pl.BlockSpec((block, LANES), lambda s, m: (s, 0))
    const = lambda shape: pl.BlockSpec(shape, lambda s, m: (0,) * len(shape))
    outs, out_specs = [], []
    if keep_psi:
        outs.append(jax.ShapeDtypeStruct((2, 1, slab, LANES, LANES), bf16))
        out_specs.append(pl.BlockSpec((2, None, planes, LANES, LANES), lambda s, m: (0, 0, s, 0, 0)))
    if ends:
        outs += [jax.ShapeDtypeStruct((band_devices, half, LANES), bf16)] * 2
        out_specs += [const(outs[-1].shape)] * 2
    else:
        outs.append(jax.ShapeDtypeStruct((rows, LANES), f32))
        out_specs.append(rowspec)
    return pl.pallas_call(
        functools.partial(inverse_kernel, groups, planes, scale, band, adds, ends, keep_psi),
        grid_spec=pltpu.PrefetchScalarGridSpec(
            num_scalar_prefetch=1,
            grid=(slab // planes,),
            in_specs=[spec] * groups
            + [pl.BlockSpec(memory_space=pltpu.SMEM), table_spec(liy), const(wiz.shape)]
            + ([rowspec] if adds else []),
            out_specs=out_specs,
            scratch_shapes=[
                pltpu.VMEM((per * groups * planes, LANES), f32),
                pltpu.VMEM((block, LANES), bf16),
            ],
        ),
        out_shape=outs,
        compiler_params=pltpu.CompilerParams(vmem_limit_bytes=16 << 20),
        cost_estimate=pl.CostEstimate(flops=10**9, bytes_accessed=4 << 20, transcendentals=0),
        name="inverse",
    )(me, *blocks, occ, liy, wiz, *([part] if adds else []))


def partner(v, axis, size, mask):
    return lax.ppermute(v, axis, [(i, i ^ mask) for i in range(size)])


def exchange(blocks, axis, size):
    if size > 4:
        index = lax.axis_index(axis)
        order = jnp.arange(size, dtype=jnp.int32) ^ index
        stacked = jnp.stack(blocks)[order]
        got = lax.all_to_all(stacked, axis, 0, 0)[order]
        return [got[m] for m in range(size)]
    return [blocks[0]] + [partner(blocks[m], axis, size, m) for m in range(1, size)]


def add_pair(mine, got):
    return (mine.astype(f32) + got.astype(f32)).astype(bf16)


def reduce_blocks(upper, lower, axis, size, fill):
    both = [upper, lower]
    steps = list(zip(*orders(size)))
    for bits in steps[:-1]:
        cut = both[0].shape[0] // 2
        got = [partner(v[cut:], axis, size, 1 << bit) for v, bit in zip(both, bits)]
        if fill is not None:
            got, fill = lax.optimization_barrier((got, fill))
            filled, fill = fill, None
        both = [add_pair(v[:cut], g) for v, g in zip(both, got)]
    mine = jnp.concatenate(both, axis=0)
    return mine, partner(mine, axis, size, 1 << steps[-1][0]), filled


def gather_blocks(both, stats, axis, size, grid, grid_size):
    steps = list(reversed(list(zip(*orders(size)))[:-1]))
    stats = sum_direct(stats, grid, range(grid_size), grid_size)
    for i, bits in enumerate(steps):
        if i:
            both = [jnp.concatenate(v, axis=0) for v in both]
            both, stats = lax.optimization_barrier((both, stats))
        both = [[v, partner(v, axis, size, 1 << bit)] for v, bit in zip(both, bits)]
    return both[0] + both[1], sum_direct(stats, axis, range(size // 2), size)


def sum_direct(v, axis, masks, size):
    if size > 8:
        for bit in range(len(masks).bit_length() - 1):
            v = v + partner(v, axis, size, 1 << bit)
        return v
    terms = [v] + [partner(v, axis, size, m) for m in masks if m]
    while len(terms) > 1:
        terms = [terms[i] + terms[i + 1] for i in range(0, len(terms), 2)]
    return terms[0]


def local(
    bands,
    occupations,
    external,
    density_in,
    prev_density,
    prev_residual,
    hist_density,
    hist_residual,
):
    groups = lax.axis_size("grid")
    band_devices = lax.axis_size("band")
    slab, ng = external.shape[:2]
    nbands = bands.shape[1]
    cells = float(ng) ** 3
    scale = density_scale / (occupations.shape[0] * band_devices)
    rows = slab * ng
    kept = ng // 2
    per = kept // groups
    wz, wiz, ly, liy, lf, li = fourier_tables(ng, groups)
    grid_at = lax.axis_index("grid").astype(jnp.int32)
    shape = (per, kept, 2 * kept)
    squared = lambda v: ((v - kept // 2) * (v - kept // 2)).astype(f32)
    place = lambda d: lax.broadcasted_iota(jnp.int32, shape, d)
    radius = squared(place(0) + grid_at * per) + squared(place(1)) + squared(place(2) % kept)
    quarter = ng / 4.0
    kinetic = jnp.exp(-time_step * radius / (quarter * quarter))
    band_at = lax.axis_index("band").astype(jnp.int32)
    me = jnp.stack([band_at, grid_at])

    flat = lambda v: v.reshape(v.shape[:-3] + (rows, ng))
    ext, rho_in, prev_in, prev_res = map(flat, (external, density_in, prev_density, prev_residual))
    hist_r, hist_q = flat(hist_density), flat(hist_residual)
    psi = [(bands, b) for b in range(nbands)]
    block = rows // band_devices
    ends = jnp.stack([band_at, band_at ^ (band_devices // 2)])
    two = lambda v, axis, at: jnp.stack(
        [lax.dynamic_slice_in_dim(v, at[i] * block, block, axis) for i in range(2)], axis=axis
    )
    hist_pair, prev_res_pair = two(hist_q, 1, ends), two(prev_res, 0, ends)
    parts = max(1, slab // 8)
    extra = []
    new_q = []
    carry = None
    mix = None
    common = dict(ext=ext, wz=wz, ly=ly)
    for iteration in range(ITERS):
        blocks = []
        for b, (array, at) in enumerate(psi):
            if iteration and b == 0:
                out = forward("mix", me, slab, groups, cells, psi=array, band=at, mix=mix, **common)
                rho_in, carry = out[groups:]
            else:
                out = forward("plain", me, slab, groups, cells, psi=array, band=at, density=rho_in, **common)
            blocks.append(exchange(out[:groups], "grid", groups))
        for b in range(nbands):
            blocks[b] = exchange(x_filter(me, blocks[b], lf, li, kinetic), "grid", groups)
        last = iteration == ITERS - 1
        part = None
        psi = []
        for b in range(nbands):
            out = inverse(
                me, blocks[b], occupations, b, nbands, liy, wiz, band_devices, scale, not last, part
            )
            if not last:
                psi.append((out[0], 0))
                out = out[1:]
            part = out[0]
        out = list(out)
        if iteration == 0:
            out[0], tie, late_in = lax.optimization_barrier((out[0], ends, prev_in))
            fill = (
                [combine(tie, hist_r, hist_q, j, parts) for j in range(DEPTH - 1)],
                late_in + mixing_weight * prev_res,
            )
        else:
            out[0], rho, prev_mid = lax.optimization_barrier((out[0], mix["rho"], mix["prev_mid"]))
            prev_mid, newest_s = middle(me, slab, rho, mix["rho_in"], prev_mid)
            fill = (orig[1:], prev_mid, extra + [newest_s])
        mine, got, fill = reduce_blocks(out[0], out[1], "band", band_devices, fill)
        orig, prev_mid = fill[:2]
        if iteration:
            extra = fill[2]
        upper, lower = finish(mine, got)
        stats, newest_q, prev_res_pair = dots(
            iteration == 0, ends, upper, lower, rho_in, prev_res_pair, hist_pair, new_q
        )
        new_q = new_q + [newest_q]
        rho, stats = gather_blocks([upper, lower], stats, "band", band_devices, "grid", groups)
        mix = dict(stats=stats, carry=carry, rho=rho, rho_in=rho_in,
                   prev_mid=prev_mid, orig=orig, extra=extra)
    density, residual = forward("last", me, slab, groups, cells, mix=mix)
    unflat = lambda v: v.reshape(slab, ng, ng)
    return unflat(density), unflat(residual)


def solution(mesh):
    placed = (
        P(None, "band", "grid", None, None),
        P("band"),
        P("grid", None, None),
        P("grid", None, None),
        P("grid", None, None),
        P("grid", None, None),
        P(None, "grid", None, None),
        P(None, "grid", None, None),
    )
    return jax.shard_map(
        local,
        mesh=mesh,
        in_specs=placed,
        out_specs=(P("grid", None, None), P("grid", None, None)),
        check_vma=False,
    )
```

profile of v0, /device:TPU:0, one launch (start us, length us, event | category | flops | bytes accessed | tf_op | source)
XLA Modules:
  0.0 252.8 jit_solution(15367720644393063326)
XLA Ops:
  3.9 2.2 copy-done.5
  7.8 2.8 %shard_map.150 = (bf16[16,32,128]{2,1,0:T(8,128)(2,1)S(1)}, bf16[16,32,128]{2,1,0:T(8,128)(2,1)S(1)}, bf16[16,32,128]{2,1,0:T(8,128)(2,1)S(1)}, bf16[16,32,128]{2,1,0:T(8,128)(2,1)S(1)}) custom-call(s32[2]{0:T(128)S(1)} %pad_add_fusion.me_ref, f32[4096,128]{1,0:T(8,128)S(1)} %bitcast.39, f32[4096,128]{1,0:T(8,128)S(1)} %bitcast.33, ...), custom_call_target="tpu_custom_call" | custom-call | flops 1000000000 | bytes 6291456 | tf_op jit(solution)/shard_map/pallas_call | solution.py:455
  11.2 2.6 %collective-permute-start.7 = (bf16[16,32,128]{2,1,0:T(8,128)(2,1)S(1)}, bf16[16,32,128]{2,1,0:T(8,128)(2,1)S(1)}, u32[]{:S(2)}, u32[]{:S(2)}) collective-permute-start(bf16[16,32,128]{2,1,0:T(8,128)(2,1)S(1)} %get-tuple-element.143), channel_id=1, source_target_pairs={{0,2},{1,3},{2,0},{3,1},{4,6},{5,7},{6,4},{7,5},{8,10},{9,11},{10,... | collective-permute-start | bytes 393224 | tf_op jit(solution)/shard_map/ppermute | solution.py:601
  13.8 2.8 %shard_map.149 = (bf16[16,32,128]{2,1,0:T(8,128)(2,1)S(1)}, bf16[16,32,128]{2,1,0:T(8,128)(2,1)S(1)}, bf16[16,32,128]{2,1,0:T(8,128)(2,1)S(1)}, bf16[16,32,128]{2,1,0:T(8,128)(2,1)S(1)}) custom-call(s32[2]{0:T(128)S(1)} %pad_add_fusion.me_ref, f32[4096,128]{1,0:T(8,128)S(1)} %bitcast.40, f32[4096,128]{1,0:T(8,128)S(1)} %bitcast.34, ...), custom_call_target="tpu_custom_call" | custom-call | flops 1000000000 | bytes 6291456 | tf_op jit(solution)/shard_map/pallas_call | solution.py:455
  16.9 1.9 collective-permute-start.1
  19.1 2.1 dynamic-slice_bitcast_fusion.1
  23.0 2.0 collective-permute-start.10
  25.0 2.0 collective-permute-done.2.refs_3_
  30.3 2.3 collective-permute-done.11.refs_3_
  32.6 2.7 %inverse.6 = (bf16[2,1,32,128,128]{4,3,2,1,0:T(8,128)(2,1)S(1)}, f32[4096,128]{1,0:T(8,128)S(1)}) custom-call(s32[2]{0:T(128)S(1)} %pad_add_fusion.me_ref, bf16[16,32,128]{2,1,0:T(8,128)(2,1)S(1)} %get-tuple-element.145.refs_0_, bf16[16,32,128]{2,1,0:T(8,128)(2,1)S(1)} %collective-permute-done.9.refs_1_, ...), custom_call_target="tpu_custom_call" | custom-call | flops 1000000000 | bytes 4194304 | tf_op jit(solution)/shard_map/inverse/pallas_call | solution.py:579
  35.5 2.7 %collective-permute-done.5.refs_3_ = bf16[16,32,128]{2,1,0:T(8,128)(2,1)S(1)} collective-permute-done((bf16[16,32,128]{2,1,0:T(8,128)(2,1)S(1)}, bf16[16,32,128]{2,1,0:T(8,128)(2,1)S(1)}, u32[]{:S(2)}, u32[]{:S(2)}) %collective-permute-start.5) | collective-permute-done | bytes 131104 | tf_op jit(solution)/shard_map/ppermute | solution.py:601
  38.2 2.8 %inverse.7 = (bf16[2,1,32,128,128]{4,3,2,1,0:T(8,128)(2,1)S(1)}, bf16[8,256,128]{2,1,0:T(8,128)(2,1)S(1)}, bf16[8,256,128]{2,1,0:T(8,128)(2,1)S(1)}) custom-call(s32[2]{0:T(128)S(1)} %pad_add_fusion.me_ref, bf16[16,32,128]{2,1,0:T(8,128)(2,1)S(1)} %get-tuple-element.137.refs_0_, bf16[16,32,128]{2,1,0:T(8,128)(2,1)S(1)} %collective-permute-done.3.refs_1_, ...), custom_call_target="tpu_custom_call" | custom-call | flops 1000000000 | bytes 4194304 | tf_op jit(solution)/shard_map/inverse/pallas_call | solution.py:579
  44.2 1.8 multiply_add_fusion.refs_6_.refs_5_
  53.0 2.9 %collective-permute-done.15 = bf16[2,256,128]{2,1,0:T(8,128)(2,1)S(1)} collective-permute-done((bf16[2,256,128]{2,1,0:T(8,128)(2,1)S(1)}, bf16[2,256,128]{2,1,0:T(8,128)(2,1)S(1)}, u32[]{:S(2)}, u32[]{:S(2)}) %collective-permute-start.15) | collective-permute-done | bytes 131104 | tf_op jit(solution)/shard_map/ppermute | solution.py:601
  57.6 3.2 %collective-permute-start.16 = (bf16[4,256,128]{2,1,0:T(8,128)(2,1)S(1)}, bf16[4,256,128]{2,1,0:T(8,128)(2,1)S(1)}, u32[]{:S(2)}, u32[]{:S(2)}) collective-permute-start(bf16[4,256,128]{2,1,0:T(8,128)(2,1)S(1)} %pad_maximum_fusion.2.mine_ref), channel_id=1, source_target_pairs={{0,16},{4,20},{8,24},{12,28},{16,0},{20,4},{24,8},{28,12},{1,17},{... | collective-permute-start | bytes 786440 | tf_op jit(solution)/shard_map/ppermute | solution.py:601
  61.1 9.2 %collective-permute-done.16.got_ref = bf16[4,256,128]{2,1,0:T(8,128)(2,1)S(1)} collective-permute-done((bf16[4,256,128]{2,1,0:T(8,128)(2,1)S(1)}, bf16[4,256,128]{2,1,0:T(8,128)(2,1)S(1)}, u32[]{:S(2)}, u32[]{:S(2)}) %collective-permute-start.16) | collective-permute-done | bytes 262176 | tf_op jit(solution)/shard_map/ppermute | solution.py:601
  70.4 2.0 dots.3
  76.1 3.5 %collective-permute-done.17 = bf16[2,256,128]{2,1,0:T(8,128)(2,1)S(1)} collective-permute-done((bf16[2,256,128]{2,1,0:T(8,128)(2,1)S(1)}, bf16[2,256,128]{2,1,0:T(8,128)(2,1)S(1)}, u32[]{:S(2)}, u32[]{:S(2)}) %collective-permute-start.17) | collective-permute-done | bytes 131104 | tf_op jit(solution)/shard_map/ppermute | solution.py:601
  81.1 1.7 collective-permute-start.26
  86.3 2.0 collective-permute-done.24
  88.7 5.1 %shard_map.151 = (bf16[16,32,128]{2,1,0:T(8,128)(2,1)S(1)}, bf16[16,32,128]{2,1,0:T(8,128)(2,1)S(1)}, bf16[16,32,128]{2,1,0:T(8,128)(2,1)S(1)}, bf16[16,32,128]{...) custom-call(s32[2]{0:T(128)S(1)} %pad_add_fusion.me_ref, f32[1,128]{1,0:T(1,128)S(1)} %add_add_fusion.4.refs_0_, ...), custom_call_target="tpu_custom_call" | custom-call | flops 1000000000 | bytes 6291456 | tf_op jit(solution)/shard_map/pallas_call | solution.py:455
  95.7 2.9 %shard_map.152 = (bf16[16,32,128]{2,1,0:T(8,128)(2,1)S(1)}, bf16[16,32,128]{2,1,0:T(8,128)(2,1)S(1)}, bf16[16,32,128]{2,1,0:T(8,128)(2,1)S(1)}, bf16[16,32,128]{2,1,0:T(8,128)(2,1)S(1)}) custom-call(s32[2]{0:T(128)S(1)} %pad_add_fusion.me_ref, f32[4096,128]{1,0:T(8,128)S(1)} %get-tuple-element.170.refs_0_.refs_2_.refs_3_.refs_6_.refs_4_, ...), custom_call_target="tpu_custom_call" | custom-call | flops 1000000000 | bytes 6291456 | tf_op jit(solution)/shard_map/pallas_call | solution.py:455
  105.9 1.7 collective-permute-done.29.refs_3_
  111.5 1.7 collective-permute-done.38.refs_3_
  113.2 2.7 %inverse.8 = (bf16[2,1,32,128,128]{4,3,2,1,0:T(8,128)(2,1)S(1)}, f32[4096,128]{1,0:T(8,128)S(1)}) custom-call(s32[2]{0:T(128)S(1)} %pad_add_fusion.me_ref, bf16[16,32,128]{2,1,0:T(8,128)(2,1)S(1)} %get-tuple-element.184.refs_0_, bf16[16,32,128]{2,1,0:T(8,128)(2,1)S(1)} %collective-permute-done.36.refs_1_, ...), custom_call_target="tpu_custom_call" | custom-call | flops 1000000000 | bytes 4194304 | tf_op jit(solution)/shard_map/inverse/pallas_call | solution.py:579
  117.1 1.7 collective-permute-done.32.refs_3_
  118.8 2.8 %inverse.9 = (bf16[2,1,32,128,128]{4,3,2,1,0:T(8,128)(2,1)S(1)}, bf16[8,256,128]{2,1,0:T(8,128)(2,1)S(1)}, bf16[8,256,128]{2,1,0:T(8,128)(2,1)S(1)}) custom-call(s32[2]{0:T(128)S(1)} %pad_add_fusion.me_ref, bf16[16,32,128]{2,1,0:T(8,128)(2,1)S(1)} %get-tuple-element.176.refs_0_, bf16[16,32,128]{2,1,0:T(8,128)(2,1)S(1)} %collective-permute-done.30.refs_1_, ...), custom_call_target="tpu_custom_call" | custom-call | flops 1000000000 | bytes 4194304 | tf_op jit(solution)/shard_map/inverse/pallas_call | solution.py:579
  125.6 4.7 %collective-permute-done.40 = bf16[4,256,128]{2,1,0:T(8,128)(2,1)S(1)} collective-permute-done((bf16[4,256,128]{2,1,0:T(8,128)(2,1)S(1)}, bf16[4,256,128]{2,1,0:T(8,128)(2,1)S(1)}, u32[]{:S(2)}, u32[]{:S(2)}) %collective-permute-start.40) | collective-permute-done | bytes 262176 | tf_op jit(solution)/shard_map/ppermute | solution.py:601
  133.7 2.8 %collective-permute-done.42 = bf16[2,256,128]{2,1,0:T(8,128)(2,1)S(1)} collective-permute-done((bf16[2,256,128]{2,1,0:T(8,128)(2,1)S(1)}, bf16[2,256,128]{2,1,0:T(8,128)(2,1)S(1)}, u32[]{:S(2)}, u32[]{:S(2)}) %collective-permute-start.42) | collective-permute-done | bytes 131104 | tf_op jit(solution)/shard_map/ppermute | solution.py:601
  139.6 11.5 %collective-permute-done.43.got_ref = bf16[4,256,128]{2,1,0:T(8,128)(2,1)S(1)} collective-permute-done((bf16[4,256,128]{2,1,0:T(8,128)(2,1)S(1)}, bf16[4,256,128]{2,1,0:T(8,128)(2,1)S(1)}, u32[]{:S(2)}, u32[]{:S(2)}) %collective-permute-start.43) | collective-permute-done | bytes 262176 | tf_op jit(solution)/shard_map/ppermute | solution.py:601
  156.4 3.6 %collective-permute-done.44 = bf16[2,256,128]{2,1,0:T(8,128)(2,1)S(1)} collective-permute-done((bf16[2,256,128]{2,1,0:T(8,128)(2,1)S(1)}, bf16[2,256,128]{2,1,0:T(8,128)(2,1)S(1)}, u32[]{:S(2)}, u32[]{:S(2)}) %collective-permute-start.44) | collective-permute-done | bytes 131104 | tf_op jit(solution)/shard_map/ppermute | solution.py:601
  160.7 1.7 collective-permute-start.53
  163.6 1.7 collective-permute-start.50
  165.9 2.9 %collective-permute-done.51 = f32[1,128]{1,0:T(1,128)S(1)} collective-permute-done((f32[1,128]{1,0:T(1,128)S(1)}, f32[1,128]{1,0:T(1,128)S(1)}, u32[]{:S(2)}, u32[]{:S(2)}) %collective-permute-start.51) | collective-permute-done | bytes 544 | tf_op jit(solution)/shard_map/ppermute | solution.py:601
  168.9 4.9 %shard_map.153 = (bf16[16,32,128]{2,1,0:T(8,128)(2,1)S(1)}, bf16[16,32,128]{2,1,0:T(8,128)(2,1)S(1)}, bf16[16,32,128]{2,1,0:T(8,128)(2,1)S(1)}, bf16[16,32,128]{...) custom-call(s32[2]{0:T(128)S(1)} %pad_add_fusion.me_ref, f32[1,128]{1,0:T(1,128)S(1)} %add_add_fusion.2.refs_0_, ...), custom_call_target="tpu_custom_call" | custom-call | flops 1000000000 | bytes 6291456 | tf_op jit(solution)/shard_map/pallas_call | solution.py:455
  175.7 3.1 %shard_map.154 = (bf16[16,32,128]{2,1,0:T(8,128)(2,1)S(1)}, bf16[16,32,128]{2,1,0:T(8,128)(2,1)S(1)}, bf16[16,32,128]{2,1,0:T(8,128)(2,1)S(1)}, bf16[16,32,128]{2,1,0:T(8,128)(2,1)S(1)}) custom-call(s32[2]{0:T(128)S(1)} %pad_add_fusion.me_ref, f32[4096,128]{1,0:T(8,128)S(1)} %get-tuple-element.217.refs_0_.refs_2_.refs_3_.refs_6_, f32[4096,128]{1,0:T(8,128)S(1)} %bitcast.38, ...), custom_call_target="tpu_custom_call" | custom-call | flops 1000000000 | bytes 6291456 | tf_op jit(solution)/shard_map/pallas_call | solution.py:455
  185.9 1.7 collective-permute-done.56.refs_3_
  191.5 1.7 collective-permute-done.65.refs_3_
  193.3 2.6 %inverse.10.refs_7_ = f32[4096,128]{1,0:T(8,128)S(1)} custom-call(s32[2]{0:T(128)S(1)} %pad_add_fusion.me_ref, bf16[16,32,128]{2,1,0:T(8,128)(2,1)S(1)} %get-tuple-element.231.refs_0_, bf16[16,32,128]{2,1,0:T(8,128)(2,1)S(1)} %collective-permute-done.63.refs_1_, bf16[16,32,128]{2,1,0:T(8,128)(2,1)S(1)} %collective-permute-done.64.refs_2_, ...), custom_call_target="tpu_custom_call" | custom-call | flops 1000000000 | bytes 4194304 | tf_op jit(solution)/shard_map/inverse/pallas_call | solution.py:579
  197.2 1.7 collective-permute-done.59.refs_3_
  198.9 2.6 %inverse.11 = (bf16[8,256,128]{2,1,0:T(8,128)(2,1)S(1)}, bf16[8,256,128]{2,1,0:T(8,128)(2,1)S(1)}) custom-call(s32[2]{0:T(128)S(1)} %pad_add_fusion.me_ref, bf16[16,32,128]{2,1,0:T(8,128)(2,1)S(1)} %get-tuple-element.223.refs_0_, bf16[16,32,128]{2,1,0:T(8,128)(2,1)S(1)} %collective-permute-done.57.refs_1_, ...), custom_call_target="tpu_custom_call" | custom-call | flops 1000000000 | bytes 4194304 | tf_op jit(solution)/shard_map/inverse/pallas_call | solution.py:579
  204.9 5.4 %collective-permute-done.67 = bf16[4,256,128]{2,1,0:T(8,128)(2,1)S(1)} collective-permute-done((bf16[4,256,128]{2,1,0:T(8,128)(2,1)S(1)}, bf16[4,256,128]{2,1,0:T(8,128)(2,1)S(1)}, u32[]{:S(2)}, u32[]{:S(2)}) %collective-permute-start.67) | collective-permute-done | bytes 262176 | tf_op jit(solution)/shard_map/ppermute | solution.py:601
  212.9 3.5 %collective-permute-done.69 = bf16[2,256,128]{2,1,0:T(8,128)(2,1)S(1)} collective-permute-done((bf16[2,256,128]{2,1,0:T(8,128)(2,1)S(1)}, bf16[2,256,128]{2,1,0:T(8,128)(2,1)S(1)}, u32[]{:S(2)}, u32[]{:S(2)}) %collective-permute-start.69) | collective-permute-done | bytes 131104 | tf_op jit(solution)/shard_map/ppermute | solution.py:601
  218.7 11.6 %collective-permute-done.70.got_ref = bf16[4,256,128]{2,1,0:T(8,128)(2,1)S(1)} collective-permute-done((bf16[4,256,128]{2,1,0:T(8,128)(2,1)S(1)}, bf16[4,256,128]{2,1,0:T(8,128)(2,1)S(1)}, u32[]{:S(2)}, u32[]{:S(2)}) %collective-permute-start.70) | collective-permute-done | bytes 262176 | tf_op jit(solution)/shard_map/ppermute | solution.py:601
  230.3 2.0 dots.5
  236.3 3.6 %collective-permute-done.71 = bf16[2,256,128]{2,1,0:T(8,128)(2,1)S(1)} collective-permute-done((bf16[2,256,128]{2,1,0:T(8,128)(2,1)S(1)}, bf16[2,256,128]{2,1,0:T(8,128)(2,1)S(1)}, u32[]{:S(2)}, u32[]{:S(2)}) %collective-permute-start.71) | collective-permute-done | bytes 131104 | tf_op jit(solution)/shard_map/ppermute | solution.py:601
  246.5 2.3 collective-permute-done.78
  248.8 3.9 %shard_map.155 = (f32[4096,128]{1,0:T(8,128)}, f32[4096,128]{1,0:T(8,128)}) custom-call(s32[2]{0:T(128)S(1)} %pad_add_fusion.me_ref, f32[1,128]{1,0:T(1,128)S(1)} %add_add_fusion.refs_0_, f32[16,128]{1,0:T(8,128)S(1)} %get-tuple-element.253.refs_1_, bf16[4,256,128]{2,1,0:T(8,128)(2,1)S(1)} %pad_maximum_fusion.9.refs_2_, ...), custom_call_target="tpu_custom_call" | custom-call | flops 1000000000 | bytes 6291456 | tf_op jit(solution)/shard_map/pallas_call | solution.py:455
  (236 shorter events, 97.8 us)
Async XLA Ops:
  10.7 10.5 %collective-permute-start.6 = (bf16[16,32,128]{2,1,0:T(8,128)(2,1)S(1)}, bf16[16,32,128]{2,1,0:T(8,128)(2,1)S(1)}, u32[]{:S(2)}, u32[]{:S(2)}) collective-permute-start(bf16[16,32,128]{2,1,0:T(8,128)(2,1)S(1)} %get-tuple-element.142), channel_id=1, source_target_pairs={{0,1},{1,0},{2,3},{3,2},{4,5},{5,4},{6,7},{7,6},{8,9},{9,8},{10,11... | collective-permute-start | bytes 393224 | tf_op jit(solution)/shard_map/ppermute | solution.py:601
  11.2 10.0 %collective-permute-start.7 = (bf16[16,32,128]{2,1,0:T(8,128)(2,1)S(1)}, bf16[16,32,128]{2,1,0:T(8,128)(2,1)S(1)}, u32[]{:S(2)}, u32[]{:S(2)}) collective-permute-start(bf16[16,32,128]{2,1,0:T(8,128)(2,1)S(1)} %get-tuple-element.143), channel_id=1, source_target_pairs={{0,2},{1,3},{2,0},{3,1},{4,6},{5,7},{6,4},{7,5},{8,10},{9,11},{10,... | collective-permute-start | bytes 393224 | tf_op jit(solution)/shard_map/ppermute | solution.py:601
  13.8 7.5 %collective-permute-start.8 = (bf16[16,32,128]{2,1,0:T(8,128)(2,1)S(1)}, bf16[16,32,128]{2,1,0:T(8,128)(2,1)S(1)}, u32[]{:S(2)}, u32[]{:S(2)}) collective-permute-start(bf16[16,32,128]{2,1,0:T(8,128)(2,1)S(1)} %get-tuple-element.144), channel_id=1, source_target_pairs={{0,3},{1,2},{2,1},{3,0},{4,7},{5,6},{6,5},{7,4},{8,11},{9,10},{10,... | collective-permute-start | bytes 393224 | tf_op jit(solution)/shard_map/ppermute | solution.py:601
  16.7 8.3 %collective-permute-start = (bf16[16,32,128]{2,1,0:T(8,128)(2,1)S(1)}, bf16[16,32,128]{2,1,0:T(8,128)(2,1)S(1)}, u32[]{:S(2)}, u32[]{:S(2)}) collective-permute-start(bf16[16,32,128]{2,1,0:T(8,128)(2,1)S(1)} %get-tuple-element.134), channel_id=1, source_target_pairs={{0,1},{1,0},{2,3},{3,2},{4,5},{5,4},{6,7},{7,6},{8,9},{9,8},{10,11... | collective-permute-start | bytes 393224 | tf_op jit(solution)/shard_map/ppermute | solution.py:601
  16.9 8.1 %collective-permute-start.1 = (bf16[16,32,128]{2,1,0:T(8,128)(2,1)S(1)}, bf16[16,32,128]{2,1,0:T(8,128)(2,1)S(1)}, u32[]{:S(2)}, u32[]{:S(2)}) collective-permute-start(bf16[16,32,128]{2,1,0:T(8,128)(2,1)S(1)} %get-tuple-element.135), channel_id=1, source_target_pairs={{0,2},{1,3},{2,0},{3,1},{4,6},{5,7},{6,4},{7,5},{8,10},{9,11},{10,... | collective-permute-start | bytes 393224 | tf_op jit(solution)/shard_map/ppermute | solution.py:601
  22.7 7.0 %collective-permute-start.9 = (bf16[16,32,128]{2,1,0:T(8,128)(2,1)S(1)}, bf16[16,32,128]{2,1,0:T(8,128)(2,1)S(1)}, u32[]{:S(2)}, u32[]{:S(2)}) collective-permute-start(bf16[16,32,128]{2,1,0:T(8,128)(2,1)S(1)} %get-tuple-element.146), channel_id=1, source_target_pairs={{0,1},{1,0},{2,3},{3,2},{4,5},{5,4},{6,7},{7,6},{8,9},{9,8},{10,11... | collective-permute-start | bytes 393224 | tf_op jit(solution)/shard_map/ppermute | solution.py:601
  23.0 7.4 %collective-permute-start.10 = (bf16[16,32,128]{2,1,0:T(8,128)(2,1)S(1)}, bf16[16,32,128]{2,1,0:T(8,128)(2,1)S(1)}, u32[]{:S(2)}, u32[]{:S(2)}) collective-permute-start(bf16[16,32,128]{2,1,0:T(8,128)(2,1)S(1)} %get-tuple-element.147), channel_id=1, source_target_pairs={{0,2},{1,3},{2,0},{3,1},{4,6},{5,7},{6,4},{7,5},{8,10},{9,11},{10,... | collective-permute-start | bytes 393224 | tf_op jit(solution)/shard_map/ppermute | solution.py:601
  25.0 7.7 %collective-permute-start.11 = (bf16[16,32,128]{2,1,0:T(8,128)(2,1)S(1)}, bf16[16,32,128]{2,1,0:T(8,128)(2,1)S(1)}, u32[]{:S(2)}, u32[]{:S(2)}) collective-permute-start(bf16[16,32,128]{2,1,0:T(8,128)(2,1)S(1)} %get-tuple-element.148), channel_id=1, source_target_pairs={{0,3},{1,2},{2,1},{3,0},{4,7},{5,6},{6,5},{7,4},{8,11},{9,10},{10,... | collective-permute-start | bytes 393224 | tf_op jit(solution)/shard_map/ppermute | solution.py:601
  28.3 7.0 %collective-permute-start.3 = (bf16[16,32,128]{2,1,0:T(8,128)(2,1)S(1)}, bf16[16,32,128]{2,1,0:T(8,128)(2,1)S(1)}, u32[]{:S(2)}, u32[]{:S(2)}) collective-permute-start(bf16[16,32,128]{2,1,0:T(8,128)(2,1)S(1)} %get-tuple-element.138), channel_id=1, source_target_pairs={{0,1},{1,0},{2,3},{3,2},{4,5},{5,4},{6,7},{7,6},{8,9},{9,8},{10,11... | collective-permute-start | bytes 393224 | tf_op jit(solution)/shard_map/ppermute | solution.py:601
  28.5 7.0 %collective-permute-start.4 = (bf16[16,32,128]{2,1,0:T(8,128)(2,1)S(1)}, bf16[16,32,128]{2,1,0:T(8,128)(2,1)S(1)}, u32[]{:S(2)}, u32[]{:S(2)}) collective-permute-start(bf16[16,32,128]{2,1,0:T(8,128)(2,1)S(1)} %get-tuple-element.139), channel_id=1, source_target_pairs={{0,2},{1,3},{2,0},{3,1},{4,6},{5,7},{6,4},{7,5},{8,10},{9,11},{10,... | collective-permute-start | bytes 393224 | tf_op jit(solution)/shard_map/ppermute | solution.py:601
  29.7 8.5 %collective-permute-start.5 = (bf16[16,32,128]{2,1,0:T(8,128)(2,1)S(1)}, bf16[16,32,128]{2,1,0:T(8,128)(2,1)S(1)}, u32[]{:S(2)}, u32[]{:S(2)}) collective-permute-start(bf16[16,32,128]{2,1,0:T(8,128)(2,1)S(1)} %get-tuple-element.140), channel_id=1, source_target_pairs={{0,3},{1,2},{2,1},{3,0},{4,7},{5,6},{6,5},{7,4},{8,11},{9,10},{10,... | collective-permute-start | bytes 393224 | tf_op jit(solution)/shard_map/ppermute | solution.py:601
  41.1 9.7 %collective-permute-start.13 = (bf16[4,256,128]{2,1,0:T(8,128)(2,1)S(1)}, bf16[4,256,128]{2,1,0:T(8,128)(2,1)S(1)}, u32[]{:S(2)}, u32[]{:S(2)}) collective-permute-start(bf16[4,256,128]{2,1,0:T(8,128)(2,1)S(1)} %slice.74), channel_id=1, source_target_pairs={{0,8},{4,12},{8,0},{12,4},{16,24},{20,28},{24,16},{28,20},{1,9},{5... | collective-permute-start | bytes 786440 | tf_op jit(solution)/shard_map/ppermute | solution.py:601
  42.7 8.1 %collective-permute-start.12 = (bf16[4,256,128]{2,1,0:T(8,128)(2,1)S(1)}, bf16[4,256,128]{2,1,0:T(8,128)(2,1)S(1)}, u32[]{:S(2)}, u32[]{:S(2)}) collective-permute-start(bf16[4,256,128]{2,1,0:T(8,128)(2,1)S(1)} %slice.73), channel_id=1, source_target_pairs={{0,4},{4,0},{8,12},{12,8},{16,20},{20,16},{24,28},{28,24},{1,5},{5... | collective-permute-start | bytes 786440 | tf_op jit(solution)/shard_map/ppermute | solution.py:601
  57.6 12.6 %collective-permute-start.16 = (bf16[4,256,128]{2,1,0:T(8,128)(2,1)S(1)}, bf16[4,256,128]{2,1,0:T(8,128)(2,1)S(1)}, u32[]{:S(2)}, u32[]{:S(2)}) collective-permute-start(bf16[4,256,128]{2,1,0:T(8,128)(2,1)S(1)} %pad_maximum_fusion.2.mine_ref), channel_id=1, source_target_pairs={{0,16},{4,20},{8,24},{12,28},{16,0},{20,4},{24,8},{28,12},{1,17},{... | collective-permute-start | bytes 786440 | tf_op jit(solution)/shard_map/ppermute | solution.py:601
  79.7 8.9 %collective-permute-start.25 = (bf16[4,256,128]{2,1,0:T(8,128)(2,1)S(1)}, bf16[4,256,128]{2,1,0:T(8,128)(2,1)S(1)}, u32[]{:S(2)}, u32[]{:S(2)}) collective-permute-start(bf16[4,256,128]{2,1,0:T(8,128)(2,1)S(1)} %pad_maximum_fusion.3.refs_1_.refs_0_), channel_id=1, source_target_pairs={{0,4},{4,0},{8,12},{12,8},{16,20},{20,16},{24,28},{28,24},{1,5},{5... | collective-permute-start | bytes 786440 | tf_op jit(solution)/shard_map/ppermute | solution.py:601
  81.1 7.5 %collective-permute-start.26 = (bf16[4,256,128]{2,1,0:T(8,128)(2,1)S(1)}, bf16[4,256,128]{2,1,0:T(8,128)(2,1)S(1)}, u32[]{:S(2)}, u32[]{:S(2)}) collective-permute-start(bf16[4,256,128]{2,1,0:T(8,128)(2,1)S(1)} %pad_maximum_fusion.4.refs_3_.refs_2_), channel_id=1, source_target_pairs={{0,8},{4,12},{8,0},{12,4},{16,24},{20,28},{24,16},{28,20},{1,9},{5... | collective-permute-start | bytes 786440 | tf_op jit(solution)/shard_map/ppermute | solution.py:601
  93.8 6.7 %collective-permute-start.34 = (bf16[16,32,128]{2,1,0:T(8,128)(2,1)S(1)}, bf16[16,32,128]{2,1,0:T(8,128)(2,1)S(1)}, u32[]{:S(2)}, u32[]{:S(2)}) collective-permute-start(bf16[16,32,128]{2,1,0:T(8,128)(2,1)S(1)} %get-tuple-element.182), channel_id=1, source_target_pairs={{0,2},{1,3},{2,0},{3,1},{4,6},{5,7},{6,4},{7,5},{8,10},{9,11},{10,... | collective-permute-start | bytes 393224 | tf_op jit(solution)/shard_map/ppermute | solution.py:601
  94.7 7.2 %collective-permute-start.35 = (bf16[16,32,128]{2,1,0:T(8,128)(2,1)S(1)}, bf16[16,32,128]{2,1,0:T(8,128)(2,1)S(1)}, u32[]{:S(2)}, u32[]{:S(2)}) collective-permute-start(bf16[16,32,128]{2,1,0:T(8,128)(2,1)S(1)} %get-tuple-element.183), channel_id=1, source_target_pairs={{0,3},{1,2},{2,1},{3,0},{4,7},{5,6},{6,5},{7,4},{8,11},{9,10},{10,... | collective-permute-start | bytes 393224 | tf_op jit(solution)/shard_map/ppermute | solution.py:601
  98.6 6.5 %collective-permute-start.27 = (bf16[16,32,128]{2,1,0:T(8,128)(2,1)S(1)}, bf16[16,32,128]{2,1,0:T(8,128)(2,1)S(1)}, u32[]{:S(2)}, u32[]{:S(2)}) collective-permute-start(bf16[16,32,128]{2,1,0:T(8,128)(2,1)S(1)} %get-tuple-element.173), channel_id=1, source_target_pairs={{0,1},{1,0},{2,3},{3,2},{4,5},{5,4},{6,7},{7,6},{8,9},{9,8},{10,11... | collective-permute-start | bytes 393224 | tf_op jit(solution)/shard_map/ppermute | solution.py:601
  99.0 6.9 %collective-permute-start.28 = (bf16[16,32,128]{2,1,0:T(8,128)(2,1)S(1)}, bf16[16,32,128]{2,1,0:T(8,128)(2,1)S(1)}, u32[]{:S(2)}, u32[]{:S(2)}) collective-permute-start(bf16[16,32,128]{2,1,0:T(8,128)(2,1)S(1)} %get-tuple-element.174), channel_id=1, source_target_pairs={{0,2},{1,3},{2,0},{3,1},{4,6},{5,7},{6,4},{7,5},{8,10},{9,11},{10,... | collective-permute-start | bytes 393224 | tf_op jit(solution)/shard_map/ppermute | solution.py:601
  99.9 7.7 %collective-permute-start.29 = (bf16[16,32,128]{2,1,0:T(8,128)(2,1)S(1)}, bf16[16,32,128]{2,1,0:T(8,128)(2,1)S(1)}, u32[]{:S(2)}, u32[]{:S(2)}) collective-permute-start(bf16[16,32,128]{2,1,0:T(8,128)(2,1)S(1)} %get-tuple-element.175), channel_id=1, source_target_pairs={{0,3},{1,2},{2,1},{3,0},{4,7},{5,6},{6,5},{7,4},{8,11},{9,10},{10,... | collective-permute-start | bytes 393224 | tf_op jit(solution)/shard_map/ppermute | solution.py:601
  103.3 7.4 %collective-permute-start.36 = (bf16[16,32,128]{2,1,0:T(8,128)(2,1)S(1)}, bf16[16,32,128]{2,1,0:T(8,128)(2,1)S(1)}, u32[]{:S(2)}, u32[]{:S(2)}) collective-permute-start(bf16[16,32,128]{2,1,0:T(8,128)(2,1)S(1)} %get-tuple-element.185), channel_id=1, source_target_pairs={{0,1},{1,0},{2,3},{3,2},{4,5},{5,4},{6,7},{7,6},{8,9},{9,8},{10,11... | collective-permute-start | bytes 393224 | tf_op jit(solution)/shard_map/ppermute | solution.py:601
  104.3 7.2 %collective-permute-start.37 = (bf16[16,32,128]{2,1,0:T(8,128)(2,1)S(1)}, bf16[16,32,128]{2,1,0:T(8,128)(2,1)S(1)}, u32[]{:S(2)}, u32[]{:S(2)}) collective-permute-start(bf16[16,32,128]{2,1,0:T(8,128)(2,1)S(1)} %get-tuple-element.186), channel_id=1, source_target_pairs={{0,2},{1,3},{2,0},{3,1},{4,6},{5,7},{6,4},{7,5},{8,10},{9,11},{10,... | collective-permute-start | bytes 393224 | tf_op jit(solution)/shard_map/ppermute | solution.py:601
  105.1 8.1 %collective-permute-start.38 = (bf16[16,32,128]{2,1,0:T(8,128)(2,1)S(1)}, bf16[16,32,128]{2,1,0:T(8,128)(2,1)S(1)}, u32[]{:S(2)}, u32[]{:S(2)}) collective-permute-start(bf16[16,32,128]{2,1,0:T(8,128)(2,1)S(1)} %get-tuple-element.187), channel_id=1, source_target_pairs={{0,3},{1,2},{2,1},{3,0},{4,7},{5,6},{6,5},{7,4},{8,11},{9,10},{10,... | collective-permute-start | bytes 393224 | tf_op jit(solution)/shard_map/ppermute | solution.py:601
  108.9 7.0 %collective-permute-start.30 = (bf16[16,32,128]{2,1,0:T(8,128)(2,1)S(1)}, bf16[16,32,128]{2,1,0:T(8,128)(2,1)S(1)}, u32[]{:S(2)}, u32[]{:S(2)}) collective-permute-start(bf16[16,32,128]{2,1,0:T(8,128)(2,1)S(1)} %get-tuple-element.177), channel_id=1, source_target_pairs={{0,1},{1,0},{2,3},{3,2},{4,5},{5,4},{6,7},{7,6},{8,9},{9,8},{10,11... | collective-permute-start | bytes 393224 | tf_op jit(solution)/shard_map/ppermute | solution.py:601
  109.9 7.2 %collective-permute-start.31 = (bf16[16,32,128]{2,1,0:T(8,128)(2,1)S(1)}, bf16[16,32,128]{2,1,0:T(8,128)(2,1)S(1)}, u32[]{:S(2)}, u32[]{:S(2)}) collective-permute-start(bf16[16,32,128]{2,1,0:T(8,128)(2,1)S(1)} %get-tuple-element.178), channel_id=1, source_target_pairs={{0,2},{1,3},{2,0},{3,1},{4,6},{5,7},{6,4},{7,5},{8,10},{9,11},{10,... | collective-permute-start | bytes 393224 | tf_op jit(solution)/shard_map/ppermute | solution.py:601
  110.7 8.1 %collective-permute-start.32 = (bf16[16,32,128]{2,1,0:T(8,128)(2,1)S(1)}, bf16[16,32,128]{2,1,0:T(8,128)(2,1)S(1)}, u32[]{:S(2)}, u32[]{:S(2)}) collective-permute-start(bf16[16,32,128]{2,1,0:T(8,128)(2,1)S(1)} %get-tuple-element.179), channel_id=1, source_target_pairs={{0,3},{1,2},{2,1},{3,0},{4,7},{5,6},{6,5},{7,4},{8,11},{9,10},{10,... | collective-permute-start | bytes 393224 | tf_op jit(solution)/shard_map/ppermute | solution.py:601
  121.7 8.6 %collective-permute-start.40 = (bf16[4,256,128]{2,1,0:T(8,128)(2,1)S(1)}, bf16[4,256,128]{2,1,0:T(8,128)(2,1)S(1)}, u32[]{:S(2)}, u32[]{:S(2)}) collective-permute-start(bf16[4,256,128]{2,1,0:T(8,128)(2,1)S(1)} %slice.82), channel_id=1, source_target_pairs={{0,8},{4,12},{8,0},{12,4},{16,24},{20,28},{24,16},{28,20},{1,9},{5... | collective-permute-start | bytes 786440 | tf_op jit(solution)/shard_map/ppermute | solution.py:601
  123.1 8.3 %collective-permute-start.39 = (bf16[4,256,128]{2,1,0:T(8,128)(2,1)S(1)}, bf16[4,256,128]{2,1,0:T(8,128)(2,1)S(1)}, u32[]{:S(2)}, u32[]{:S(2)}) collective-permute-start(bf16[4,256,128]{2,1,0:T(8,128)(2,1)S(1)} %slice.81), channel_id=1, source_target_pairs={{0,4},{4,0},{8,12},{12,8},{16,20},{20,16},{24,28},{28,24},{1,5},{5... | collective-permute-start | bytes 786440 | tf_op jit(solution)/shard_map/ppermute | solution.py:601
  138.2 12.9 %collective-permute-start.43 = (bf16[4,256,128]{2,1,0:T(8,128)(2,1)S(1)}, bf16[4,256,128]{2,1,0:T(8,128)(2,1)S(1)}, u32[]{:S(2)}, u32[]{:S(2)}) collective-permute-start(bf16[4,256,128]{2,1,0:T(8,128)(2,1)S(1)} %pad_maximum_fusion.5.mine_ref), channel_id=1, source_target_pairs={{0,16},{4,20},{8,24},{12,28},{16,0},{20,4},{24,8},{28,12},{1,17},{... | collective-permute-start | bytes 786440 | tf_op jit(solution)/shard_map/ppermute | solution.py:601
  160.0 8.9 %collective-permute-start.52 = (bf16[4,256,128]{2,1,0:T(8,128)(2,1)S(1)}, bf16[4,256,128]{2,1,0:T(8,128)(2,1)S(1)}, u32[]{:S(2)}, u32[]{:S(2)}) collective-permute-start(bf16[4,256,128]{2,1,0:T(8,128)(2,1)S(1)} %pad_maximum_fusion.6.refs_2_.refs_0_), channel_id=1, source_target_pairs={{0,4},{4,0},{8,12},{12,8},{16,20},{20,16},{24,28},{28,24},{1,5},{5... | collective-permute-start | bytes 786440 | tf_op jit(solution)/shard_map/ppermute | solution.py:601
  160.7 8.2 %collective-permute-start.53 = (bf16[4,256,128]{2,1,0:T(8,128)(2,1)S(1)}, bf16[4,256,128]{2,1,0:T(8,128)(2,1)S(1)}, u32[]{:S(2)}, u32[]{:S(2)}) collective-permute-start(bf16[4,256,128]{2,1,0:T(8,128)(2,1)S(1)} %pad_maximum_fusion.7.refs_4_.refs_2_), channel_id=1, source_target_pairs={{0,8},{4,12},{8,0},{12,4},{16,24},{20,28},{24,16},{28,20},{1,9},{5... | collective-permute-start | bytes 786440 | tf_op jit(solution)/shard_map/ppermute | solution.py:601
  162.4 6.4 %collective-permute-start.51 = (f32[1,128]{1,0:T(1,128)S(1)}, f32[1,128]{1,0:T(1,128)S(1)}, u32[]{:S(2)}, u32[]{:S(2)}) collective-permute-start(f32[1,128]{1,0:T(1,128)S(1)} %add_add_fusion.3), channel_id=1, source_target_pairs={{0,12},{4,8},{8,4},{12,0},{16,28},{20,24},{24,20},{28,16},{1,13},{... | collective-permute-start | bytes 1544 | tf_op jit(solution)/shard_map/ppermute | solution.py:601
  173.9 6.9 %collective-permute-start.61 = (bf16[16,32,128]{2,1,0:T(8,128)(2,1)S(1)}, bf16[16,32,128]{2,1,0:T(8,128)(2,1)S(1)}, u32[]{:S(2)}, u32[]{:S(2)}) collective-permute-start(bf16[16,32,128]{2,1,0:T(8,128)(2,1)S(1)} %get-tuple-element.229), channel_id=1, source_target_pairs={{0,2},{1,3},{2,0},{3,1},{4,6},{5,7},{6,4},{7,5},{8,10},{9,11},{10,... | collective-permute-start | bytes 393224 | tf_op jit(solution)/shard_map/ppermute | solution.py:601
  174.7 7.3 %collective-permute-start.62 = (bf16[16,32,128]{2,1,0:T(8,128)(2,1)S(1)}, bf16[16,32,128]{2,1,0:T(8,128)(2,1)S(1)}, u32[]{:S(2)}, u32[]{:S(2)}) collective-permute-start(bf16[16,32,128]{2,1,0:T(8,128)(2,1)S(1)} %get-tuple-element.230), channel_id=1, source_target_pairs={{0,3},{1,2},{2,1},{3,0},{4,7},{5,6},{6,5},{7,4},{8,11},{9,10},{10,... | collective-permute-start | bytes 393224 | tf_op jit(solution)/shard_map/ppermute | solution.py:601
  179.3 6.6 %collective-permute-start.55 = (bf16[16,32,128]{2,1,0:T(8,128)(2,1)S(1)}, bf16[16,32,128]{2,1,0:T(8,128)(2,1)S(1)}, u32[]{:S(2)}, u32[]{:S(2)}) collective-permute-start(bf16[16,32,128]{2,1,0:T(8,128)(2,1)S(1)} %get-tuple-element.221), channel_id=1, source_target_pairs={{0,2},{1,3},{2,0},{3,1},{4,6},{5,7},{6,4},{7,5},{8,10},{9,11},{10,... | collective-permute-start | bytes 393224 | tf_op jit(solution)/shard_map/ppermute | solution.py:601
  180.1 7.6 %collective-permute-start.56 = (bf16[16,32,128]{2,1,0:T(8,128)(2,1)S(1)}, bf16[16,32,128]{2,1,0:T(8,128)(2,1)S(1)}, u32[]{:S(2)}, u32[]{:S(2)}) collective-permute-start(bf16[16,32,128]{2,1,0:T(8,128)(2,1)S(1)} %get-tuple-element.222), channel_id=1, source_target_pairs={{0,3},{1,2},{2,1},{3,0},{4,7},{5,6},{6,5},{7,4},{8,11},{9,10},{10,... | collective-permute-start | bytes 393224 | tf_op jit(solution)/shard_map/ppermute | solution.py:601
  183.3 7.4 %collective-permute-start.63 = (bf16[16,32,128]{2,1,0:T(8,128)(2,1)S(1)}, bf16[16,32,128]{2,1,0:T(8,128)(2,1)S(1)}, u32[]{:S(2)}, u32[]{:S(2)}) collective-permute-start(bf16[16,32,128]{2,1,0:T(8,128)(2,1)S(1)} %get-tuple-element.232), channel_id=1, source_target_pairs={{0,1},{1,0},{2,3},{3,2},{4,5},{5,4},{6,7},{7,6},{8,9},{9,8},{10,11... | collective-permute-start | bytes 393224 | tf_op jit(solution)/shard_map/ppermute | solution.py:601
  184.3 7.2 %collective-permute-start.64 = (bf16[16,32,128]{2,1,0:T(8,128)(2,1)S(1)}, bf16[16,32,128]{2,1,0:T(8,128)(2,1)S(1)}, u32[]{:S(2)}, u32[]{:S(2)}) collective-permute-start(bf16[16,32,128]{2,1,0:T(8,128)(2,1)S(1)} %get-tuple-element.233), channel_id=1, source_target_pairs={{0,2},{1,3},{2,0},{3,1},{4,6},{5,7},{6,4},{7,5},{8,10},{9,11},{10,... | collective-permute-start | bytes 393224 | tf_op jit(solution)/shard_map/ppermute | solution.py:601
  185.1 8.2 %collective-permute-start.65 = (bf16[16,32,128]{2,1,0:T(8,128)(2,1)S(1)}, bf16[16,32,128]{2,1,0:T(8,128)(2,1)S(1)}, u32[]{:S(2)}, u32[]{:S(2)}) collective-permute-start(bf16[16,32,128]{2,1,0:T(8,128)(2,1)S(1)} %get-tuple-element.234), channel_id=1, source_target_pairs={{0,3},{1,2},{2,1},{3,0},{4,7},{5,6},{6,5},{7,4},{8,11},{9,10},{10,... | collective-permute-start | bytes 393224 | tf_op jit(solution)/shard_map/ppermute | solution.py:601
  189.0 6.9 %collective-permute-start.57 = (bf16[16,32,128]{2,1,0:T(8,128)(2,1)S(1)}, bf16[16,32,128]{2,1,0:T(8,128)(2,1)S(1)}, u32[]{:S(2)}, u32[]{:S(2)}) collective-permute-start(bf16[16,32,128]{2,1,0:T(8,128)(2,1)S(1)} %get-tuple-element.224), channel_id=1, source_target_pairs={{0,1},{1,0},{2,3},{3,2},{4,5},{5,4},{6,7},{7,6},{8,9},{9,8},{10,11... | collective-permute-start | bytes 393224 | tf_op jit(solution)/shard_map/ppermute | solution.py:601
  189.9 7.2 %collective-permute-start.58 = (bf16[16,32,128]{2,1,0:T(8,128)(2,1)S(1)}, bf16[16,32,128]{2,1,0:T(8,128)(2,1)S(1)}, u32[]{:S(2)}, u32[]{:S(2)}) collective-permute-start(bf16[16,32,128]{2,1,0:T(8,128)(2,1)S(1)} %get-tuple-element.225), channel_id=1, source_target_pairs={{0,2},{1,3},{2,0},{3,1},{4,6},{5,7},{6,4},{7,5},{8,10},{9,11},{10,... | collective-permute-start | bytes 393224 | tf_op jit(solution)/shard_map/ppermute | solution.py:601
  190.7 8.2 %collective-permute-start.59 = (bf16[16,32,128]{2,1,0:T(8,128)(2,1)S(1)}, bf16[16,32,128]{2,1,0:T(8,128)(2,1)S(1)}, u32[]{:S(2)}, u32[]{:S(2)}) collective-permute-start(bf16[16,32,128]{2,1,0:T(8,128)(2,1)S(1)} %get-tuple-element.226), channel_id=1, source_target_pairs={{0,3},{1,2},{2,1},{3,0},{4,7},{5,6},{6,5},{7,4},{8,11},{9,10},{10,... | collective-permute-start | bytes 393224 | tf_op jit(solution)/shard_map/ppermute | solution.py:601
  201.6 8.6 %collective-permute-start.67 = (bf16[4,256,128]{2,1,0:T(8,128)(2,1)S(1)}, bf16[4,256,128]{2,1,0:T(8,128)(2,1)S(1)}, u32[]{:S(2)}, u32[]{:S(2)}) collective-permute-start(bf16[4,256,128]{2,1,0:T(8,128)(2,1)S(1)} %slice.90), channel_id=1, source_target_pairs={{0,8},{4,12},{8,0},{12,4},{16,24},{20,28},{24,16},{28,20},{1,9},{5... | collective-permute-start | bytes 786440 | tf_op jit(solution)/shard_map/ppermute | solution.py:601
  203.1 8.3 %collective-permute-start.66 = (bf16[4,256,128]{2,1,0:T(8,128)(2,1)S(1)}, bf16[4,256,128]{2,1,0:T(8,128)(2,1)S(1)}, u32[]{:S(2)}, u32[]{:S(2)}) collective-permute-start(bf16[4,256,128]{2,1,0:T(8,128)(2,1)S(1)} %slice.89), channel_id=1, source_target_pairs={{0,4},{4,0},{8,12},{12,8},{16,20},{20,16},{24,28},{28,24},{1,5},{5... | collective-permute-start | bytes 786440 | tf_op jit(solution)/shard_map/ppermute | solution.py:601
  217.4 12.9 %collective-permute-start.70 = (bf16[4,256,128]{2,1,0:T(8,128)(2,1)S(1)}, bf16[4,256,128]{2,1,0:T(8,128)(2,1)S(1)}, u32[]{:S(2)}, u32[]{:S(2)}) collective-permute-start(bf16[4,256,128]{2,1,0:T(8,128)(2,1)S(1)} %pad_maximum_fusion.8.mine_ref), channel_id=1, source_target_pairs={{0,16},{4,20},{8,24},{12,28},{16,0},{20,4},{24,8},{28,12},{1,17},{... | collective-permute-start | bytes 786440 | tf_op jit(solution)/shard_map/ppermute | solution.py:601
  239.9 8.9 %collective-permute-start.79 = (bf16[4,256,128]{2,1,0:T(8,128)(2,1)S(1)}, bf16[4,256,128]{2,1,0:T(8,128)(2,1)S(1)}, u32[]{:S(2)}, u32[]{:S(2)}) collective-permute-start(bf16[4,256,128]{2,1,0:T(8,128)(2,1)S(1)} %pad_maximum_fusion.9.refs_2_), channel_id=1, source_target_pairs={{0,4},{4,0},{8,12},{12,8},{16,20},{20,16},{24,28},{28,24},{1,5},{5... | collective-permute-start | bytes 786440 | tf_op jit(solution)/shard_map/ppermute | solution.py:601
  241.3 7.5 %collective-permute-start.80 = (bf16[4,256,128]{2,1,0:T(8,128)(2,1)S(1)}, bf16[4,256,128]{2,1,0:T(8,128)(2,1)S(1)}, u32[]{:S(2)}, u32[]{:S(2)}) collective-permute-start(bf16[4,256,128]{2,1,0:T(8,128)(2,1)S(1)} %pad_maximum_fusion.10.refs_4_), channel_id=1, source_target_pairs={{0,8},{4,12},{8,0},{12,4},{16,24},{20,28},{24,16},{28,20},{1,9},{5... | collective-permute-start | bytes 786440 | tf_op jit(solution)/shard_map/ppermute | solution.py:601
  (52 other events, 344.0 us)
where the time goes:
time: 253 us
  waiting for transfers between devices  102 us (40%)
  starting transfers between devices  74.3 us (29%)
  Pallas kernels  62.1 us (25%)
  local copies, waits for them, and re-layouts  9.48 us (4%)
  other arithmetic  3.27 us (1%)
    ppermute x81, waiting for transfers between devices, partner(): return lax.ppermute(v, axis, [(i, i ^ mask) for i in range(size)])  102 us
    ppermute x81, starting transfers between devices, partner(): return lax.ppermute(v, axis, [(i, i ^ mask) for i in range(size)])  74.3 us
    pallas_call x7, Pallas kernels, forward(): pl.pallas_call(functools.partial(forward_kernel, kind, planes, first, gro...  25.6 us
    pallas_call x6, Pallas kernels, inverse(): pl.pallas_call(functools.partial(inverse_kernel, groups, planes, scale, b...  16.2 us
    pallas_call x6, Pallas kernels, x_filter(): pl.pallas_call(functools.partial(filter_kernel, groups), grid_spec=pltpu....  7.88 us
    unnamed x38, local copies, waits for them, and re-layouts  7.2 us
    pallas_call x3, Pallas kernels, dots(): pl.pallas_call(functools.partial(dots_kernel, first), grid_spec=pltpu.Pre...  5.27 us
  transfers between devices with their start and end apart: 81, of which 42 were waited for; matrix products, arithmetic and copies ran while one was open for 2% of the time, Pallas kernels for 13%

commit v1 on v0

--- a/solution.py
+++ b/solution.py
@@ -239,16 +239,15 @@
     return jnp.sum(v, axis=0, keepdims=True)
 
 
-def finish_kernel(mine_ref, got_ref, upper_ref, lower_ref):
-    for i in range(4):
-        v = (mine_ref[i].astype(f32) + got_ref[i ^ 1].astype(f32)).astype(bf16)
-        (upper_ref, lower_ref)[i // 2][i % 2] = v
+def finish_kernel(mine_ref, got_ref, sum_ref):
+    for i in range(2):
+        sum_ref[i] = (mine_ref[i].astype(f32) + got_ref[1 - i].astype(f32)).astype(bf16)
 
 
 def finish(mine, got):
     return pl.pallas_call(
         finish_kernel,
-        out_shape=[jax.ShapeDtypeStruct((2,) + mine.shape[1:], bf16)] * 2,
+        out_shape=jax.ShapeDtypeStruct(mine.shape, bf16),
         compiler_params=pltpu.CompilerParams(vmem_limit_bytes=8 << 20),
         cost_estimate=pl.CostEstimate(flops=10**6, bytes_accessed=3 * mine.size, transcendentals=0),
         name="finish",
@@ -625,8 +624,7 @@
             got, fill = lax.optimization_barrier((got, fill))
             filled, fill = fill, None
         both = [add_pair(v[:cut], g) for v, g in zip(both, got)]
-    mine = jnp.concatenate(both, axis=0)
-    return mine, partner(mine, axis, size, 1 << steps[-1][0]), filled
+    return both, [partner(v, axis, size, 1 << bit) for v, bit in zip(both, steps[-1])], filled
 
 
 def gather_blocks(both, stats, axis, size, grid, grid_size):
@@ -734,7 +732,7 @@
         orig, prev_mid = fill[:2]
         if iteration:
             extra = fill[2]
-        upper, lower = finish(mine, got)
+        upper, lower = (finish(m, g) for m, g in zip(mine, got))
         stats, newest_q, prev_res_pair = dots(
             iteration == 0, ends, upper, lower, rho_in, prev_res_pair, hist_pair, new_q
         )

time: 253 us -> 251 us (level)
  waiting for transfers between devices: 102 us -> 95.9 us
  starting transfers between devices: 74.3 us -> 77.2 us
    ppermute x81 -> x84, waiting for transfers between devices: 102 us -> 95.9 us  [partner(): return lax.ppermute(v, axis, [(i, i ^ mask) for i in range(size)])]
    ppermute x81 -> x84, starting transfers between devices: 74.3 us -> 77.2 us  [partner(): return lax.ppermute(v, axis, [(i, i ^ mask) for i in range(size)])]
    unnamed x38 -> x44, local copies, waits for them, and re-layouts: 7.2 us -> 7.2 us
  transfers between devices with their start and end apart: 81 -> 84, of which waited for: 42 -> 45; matrix products, arithmetic and copies ran while one was open for 2% -> 2% of each run, Pallas kernels for 13% -> 13%
where the time goes in v1:
time: 251 us; the launch traced here: 250 us
  waiting for transfers between devices  95.9 us (38%)
  starting transfers between devices  77.2 us (31%)
  Pallas kernels  62.7 us (25%)
  local copies, waits for them, and re-layouts  9.49 us (4%)
  other arithmetic  3.65 us (1%)
    ppermute x84, waiting for transfers between devices, partner(): return lax.ppermute(v, axis, [(i, i ^ mask) for i in range(size)])  95.9 us
    ppermute x84, starting transfers between devices, partner(): return lax.ppermute(v, axis, [(i, i ^ mask) for i in range(size)])  77.2 us
    pallas_call x7, Pallas kernels, forward(): pl.pallas_call(functools.partial(forward_kernel, kind, planes, first, gro...  26.3 us
    pallas_call x6, Pallas kernels, inverse(): pl.pallas_call(functools.partial(inverse_kernel, groups, planes, scale, b...  16.2 us
    pallas_call x6, Pallas kernels, x_filter(): pl.pallas_call(functools.partial(filter_kernel, groups), grid_spec=pltpu....  7.87 us
    unnamed x44, local copies, waits for them, and re-layouts  7.2 us
    pallas_call x3, Pallas kernels, dots(): pl.pallas_call(functools.partial(dots_kernel, first), grid_spec=pltpu.Pre...  5.18 us
  transfers between devices with their start and end apart: 84, of which 45 were waited for; matrix products, arithmetic and copies ran while one was open for 2% of the time, Pallas kernels for 13%

profile of v1, /device:TPU:0, one launch (start us, length us, event | category | flops | bytes accessed | tf_op | source)
XLA Modules:
  0.0 250.3 jit_solution(16537350191373430157)
XLA Ops:
  3.9 2.2 copy-done.4
  7.8 3.5 %shard_map.150 = (bf16[16,32,128]{2,1,0:T(8,128)(2,1)S(1)}, bf16[16,32,128]{2,1,0:T(8,128)(2,1)}, bf16[16,32,128]{2,1,0:T(8,128)(2,1)}, bf16[16,32,128]{2,1,0:T(8,128)(2,1)S(1)}) custom-call(s32[2]{0:T(128)S(1)} %pad_add_fusion.me_ref, f32[4096,128]{1,0:T(8,128)S(1)} %bitcast.41, f32[4096,128]{1,0:T(8,128)S(1)} %bitcast.35, ...), custom_call_target="tpu_custom_call" | custom-call | flops 1000000000 | bytes 6291456 | tf_op jit(solution)/shard_map/pallas_call | solution.py:454
  11.8 2.5 collective-permute-start.7
  14.4 2.8 %shard_map.149 = (bf16[16,32,128]{2,1,0:T(8,128)(2,1)S(1)}, bf16[16,32,128]{2,1,0:T(8,128)(2,1)S(1)}, bf16[16,32,128]{2,1,0:T(8,128)(2,1)S(1)}, bf16[16,32,128]{2,1,0:T(8,128)(2,1)S(1)}) custom-call(s32[2]{0:T(128)S(1)} %pad_add_fusion.me_ref, f32[4096,128]{1,0:T(8,128)S(1)} %bitcast.42, f32[4096,128]{1,0:T(8,128)S(1)} %bitcast.36, ...), custom_call_target="tpu_custom_call" | custom-call | flops 1000000000 | bytes 6291456 | tf_op jit(solution)/shard_map/pallas_call | solution.py:454
  17.4 1.9 collective-permute-start.1
  21.3 2.1 dynamic-slice_bitcast_fusion.1
  25.4 2.0 collective-permute-start.10
  27.3 1.8 collective-permute-done.2.refs_3_
  32.4 2.3 collective-permute-done.11.refs_3_
  34.7 2.7 %inverse.6 = (bf16[2,1,32,128,128]{4,3,2,1,0:T(8,128)(2,1)S(1)}, f32[4096,128]{1,0:T(8,128)S(1)}) custom-call(s32[2]{0:T(128)S(1)} %pad_add_fusion.me_ref, bf16[16,32,128]{2,1,0:T(8,128)(2,1)S(1)} %get-tuple-element.139.refs_0_, bf16[16,32,128]{2,1,0:T(8,128)(2,1)S(1)} %collective-permute-done.9.refs_1_, ...), custom_call_target="tpu_custom_call" | custom-call | flops 1000000000 | bytes 4194304 | tf_op jit(solution)/shard_map/inverse/pallas_call | solution.py:578
  37.8 2.6 %collective-permute-done.5.refs_3_ = bf16[16,32,128]{2,1,0:T(8,128)(2,1)S(1)} collective-permute-done((bf16[16,32,128]{2,1,0:T(8,128)(2,1)S(1)}, bf16[16,32,128]{2,1,0:T(8,128)(2,1)S(1)}, u32[]{:S(2)}, u32[]{:S(2)}) %collective-permute-start.5) | collective-permute-done | bytes 131104 | tf_op jit(solution)/shard_map/ppermute | solution.py:600
  40.3 2.8 %inverse.7 = (bf16[2,1,32,128,128]{4,3,2,1,0:T(8,128)(2,1)S(1)}, bf16[8,256,128]{2,1,0:T(8,128)(2,1)S(1)}, bf16[8,256,128]{2,1,0:T(8,128)(2,1)S(1)}) custom-call(s32[2]{0:T(128)S(1)} %pad_add_fusion.me_ref, bf16[16,32,128]{2,1,0:T(8,128)(2,1)S(1)} %get-tuple-element.131.refs_0_, bf16[16,32,128]{2,1,0:T(8,128)(2,1)S(1)} %collective-permute-done.3.refs_1_, ...), custom_call_target="tpu_custom_call" | custom-call | flops 1000000000 | bytes 4194304 | tf_op jit(solution)/shard_map/inverse/pallas_call | solution.py:578
  55.1 2.8 %collective-permute-done.17 = bf16[2,256,128]{2,1,0:T(8,128)(2,1)S(1)} collective-permute-done((bf16[2,256,128]{2,1,0:T(8,128)(2,1)S(1)}, bf16[2,256,128]{2,1,0:T(8,128)(2,1)S(1)}, u32[]{:S(2)}, u32[]{:S(2)}) %collective-permute-start.17) | collective-permute-done | bytes 131104 | tf_op jit(solution)/shard_map/ppermute | solution.py:600
  58.0 2.7 %collective-permute-start.18 = (bf16[2,256,128]{2,1,0:T(8,128)(2,1)S(1)}, bf16[2,256,128]{2,1,0:T(8,128)(2,1)S(1)}, u32[]{:S(2)}, u32[]{:S(2)}) collective-permute-start(bf16[2,256,128]{2,1,0:T(8,128)(2,1)S(1)} %add_convert_fusion.10.mine_ref), channel_id=1, source_target_pairs={{0,16},{4,20},{8,24},{12,28},{16,0},{20,4},{24,8},{28,12},{1,17},{... | collective-permute-start | bytes 393224 | tf_op jit(solution)/shard_map/ppermute | solution.py:600
  60.7 2.6 %collective-permute-start.15 = (bf16[2,256,128]{2,1,0:T(8,128)(2,1)S(1)}, bf16[2,256,128]{2,1,0:T(8,128)(2,1)S(1)}, u32[]{:S(2)}, u32[]{:S(2)}) collective-permute-start(bf16[2,256,128]{2,1,0:T(8,128)(2,1)S(1)} %add_convert_fusion.11.mine_ref), channel_id=1, source_target_pairs={{0,16},{4,20},{8,24},{12,28},{16,0},{20,4},{24,8},{28,12},{1,17},{... | collective-permute-start | bytes 393224 | tf_op jit(solution)/shard_map/ppermute | solution.py:600
  63.3 5.8 %collective-permute-done.18.got_ref = bf16[2,256,128]{2,1,0:T(8,128)(2,1)S(1)} collective-permute-done((bf16[2,256,128]{2,1,0:T(8,128)(2,1)S(1)}, bf16[2,256,128]{2,1,0:T(8,128)(2,1)S(1)}, u32[]{:S(2)}, u32[]{:S(2)}) %collective-permute-start.18) | collective-permute-done | bytes 131104 | tf_op jit(solution)/shard_map/ppermute | solution.py:600
  70.7 1.9 dots.3
  76.3 3.9 %collective-permute-done.19 = bf16[2,256,128]{2,1,0:T(8,128)(2,1)S(1)} collective-permute-done((bf16[2,256,128]{2,1,0:T(8,128)(2,1)S(1)}, bf16[2,256,128]{2,1,0:T(8,128)(2,1)S(1)}, u32[]{:S(2)}, u32[]{:S(2)}) %collective-permute-start.19) | collective-permute-done | bytes 131104 | tf_op jit(solution)/shard_map/ppermute | solution.py:600
  82.3 2.7 %collective-permute-start.25 = (f32[1,128]{1,0:T(1,128)S(1)}, f32[1,128]{1,0:T(1,128)S(1)}, u32[]{:S(2)}, u32[]{:S(2)}) collective-permute-start(f32[1,128]{1,0:T(1,128)S(1)} %add_add_fusion.5), channel_id=1, source_target_pairs={{0,12},{4,8},{8,4},{12,0},{16,28},{20,24},{24,20},{28,16},{1,13},{... | collective-permute-start | bytes 1544 | tf_op jit(solution)/shard_map/ppermute | solution.py:600
  85.8 4.3 %collective-permute-done.25 = f32[1,128]{1,0:T(1,128)S(1)} collective-permute-done((f32[1,128]{1,0:T(1,128)S(1)}, f32[1,128]{1,0:T(1,128)S(1)}, u32[]{:S(2)}, u32[]{:S(2)}) %collective-permute-start.25) | collective-permute-done | bytes 544 | tf_op jit(solution)/shard_map/ppermute | solution.py:600
  90.2 5.1 %shard_map.151 = (bf16[16,32,128]{2,1,0:T(8,128)(2,1)S(1)}, bf16[16,32,128]{2,1,0:T(8,128)(2,1)S(1)}, bf16[16,32,128]{2,1,0:T(8,128)(2,1)S(1)}, bf16[16,32,128]{...) custom-call(s32[2]{0:T(128)S(1)} %pad_add_fusion.me_ref, f32[1,128]{1,0:T(1,128)S(1)} %add_add_fusion.4.refs_0_, ...), custom_call_target="tpu_custom_call" | custom-call | flops 1000000000 | bytes 6291456 | tf_op jit(solution)/shard_map/pallas_call | solution.py:454
  97.2 2.9 %shard_map.152 = (bf16[16,32,128]{2,1,0:T(8,128)(2,1)S(1)}, bf16[16,32,128]{2,1,0:T(8,128)(2,1)S(1)}, bf16[16,32,128]{2,1,0:T(8,128)(2,1)S(1)}, bf16[16,32,128]{2,1,0:T(8,128)(2,1)S(1)}) custom-call(s32[2]{0:T(128)S(1)} %pad_add_fusion.me_ref, f32[4096,128]{1,0:T(8,128)S(1)} %get-tuple-element.162.refs_0_.refs_2_.refs_3_.refs_6_.refs_4_, ...), custom_call_target="tpu_custom_call" | custom-call | flops 1000000000 | bytes 6291456 | tf_op jit(solution)/shard_map/pallas_call | solution.py:454
  107.4 1.7 collective-permute-done.30.refs_3_
  113.0 1.7 collective-permute-done.39.refs_3_
  114.7 2.7 %inverse.8 = (bf16[2,1,32,128,128]{4,3,2,1,0:T(8,128)(2,1)S(1)}, f32[4096,128]{1,0:T(8,128)S(1)}) custom-call(s32[2]{0:T(128)S(1)} %pad_add_fusion.me_ref, bf16[16,32,128]{2,1,0:T(8,128)(2,1)S(1)} %get-tuple-element.176.refs_0_, bf16[16,32,128]{2,1,0:T(8,128)(2,1)S(1)} %collective-permute-done.37.refs_1_, ...), custom_call_target="tpu_custom_call" | custom-call | flops 1000000000 | bytes 4194304 | tf_op jit(solution)/shard_map/inverse/pallas_call | solution.py:578
  120.3 2.8 %inverse.9 = (bf16[2,1,32,128,128]{4,3,2,1,0:T(8,128)(2,1)S(1)}, bf16[8,256,128]{2,1,0:T(8,128)(2,1)S(1)}, bf16[8,256,128]{2,1,0:T(8,128)(2,1)S(1)}) custom-call(s32[2]{0:T(128)S(1)} %pad_add_fusion.me_ref, bf16[16,32,128]{2,1,0:T(8,128)(2,1)S(1)} %get-tuple-element.168.refs_0_, bf16[16,32,128]{2,1,0:T(8,128)(2,1)S(1)} %collective-permute-done.31.refs_1_, ...), custom_call_target="tpu_custom_call" | custom-call | flops 1000000000 | bytes 4194304 | tf_op jit(solution)/shard_map/inverse/pallas_call | solution.py:578
  125.6 6.2 %collective-permute-done.41 = bf16[4,256,128]{2,1,0:T(8,128)(2,1)S(1)} collective-permute-done((bf16[4,256,128]{2,1,0:T(8,128)(2,1)S(1)}, bf16[4,256,128]{2,1,0:T(8,128)(2,1)S(1)}, u32[]{:S(2)}, u32[]{:S(2)}) %collective-permute-start.41) | collective-permute-done | bytes 262176 | tf_op jit(solution)/shard_map/ppermute | solution.py:600
  134.5 2.7 %collective-permute-done.45 = bf16[2,256,128]{2,1,0:T(8,128)(2,1)S(1)} collective-permute-done((bf16[2,256,128]{2,1,0:T(8,128)(2,1)S(1)}, bf16[2,256,128]{2,1,0:T(8,128)(2,1)S(1)}, u32[]{:S(2)}, u32[]{:S(2)}) %collective-permute-start.45) | collective-permute-done | bytes 131104 | tf_op jit(solution)/shard_map/ppermute | solution.py:600
  137.3 2.9 %collective-permute-start.46 = (bf16[2,256,128]{2,1,0:T(8,128)(2,1)S(1)}, bf16[2,256,128]{2,1,0:T(8,128)(2,1)S(1)}, u32[]{:S(2)}, u32[]{:S(2)}) collective-permute-start(bf16[2,256,128]{2,1,0:T(8,128)(2,1)S(1)} %add_convert_fusion.8.mine_ref), channel_id=1, source_target_pairs={{0,16},{4,20},{8,24},{12,28},{16,0},{20,4},{24,8},{28,12},{1,17},{... | collective-permute-start | bytes 393224 | tf_op jit(solution)/shard_map/ppermute | solution.py:600
  141.5 7.4 %collective-permute-done.46.got_ref = bf16[2,256,128]{2,1,0:T(8,128)(2,1)S(1)} collective-permute-done((bf16[2,256,128]{2,1,0:T(8,128)(2,1)S(1)}, bf16[2,256,128]{2,1,0:T(8,128)(2,1)S(1)}, u32[]{:S(2)}, u32[]{:S(2)}) %collective-permute-start.46) | collective-permute-done | bytes 131104 | tf_op jit(solution)/shard_map/ppermute | solution.py:600
  155.3 3.6 %collective-permute-done.47 = bf16[2,256,128]{2,1,0:T(8,128)(2,1)S(1)} collective-permute-done((bf16[2,256,128]{2,1,0:T(8,128)(2,1)S(1)}, bf16[2,256,128]{2,1,0:T(8,128)(2,1)S(1)}, u32[]{:S(2)}, u32[]{:S(2)}) %collective-permute-start.47) | collective-permute-done | bytes 131104 | tf_op jit(solution)/shard_map/ppermute | solution.py:600
  161.0 2.0 collective-permute-start.53
  164.5 3.3 %collective-permute-done.53 = f32[1,128]{1,0:T(1,128)S(1)} collective-permute-done((f32[1,128]{1,0:T(1,128)S(1)}, f32[1,128]{1,0:T(1,128)S(1)}, u32[]{:S(2)}, u32[]{:S(2)}) %collective-permute-start.53) | collective-permute-done | bytes 544 | tf_op jit(solution)/shard_map/ppermute | solution.py:600
  167.9 4.9 %shard_map.153 = (bf16[16,32,128]{2,1,0:T(8,128)(2,1)S(1)}, bf16[16,32,128]{2,1,0:T(8,128)(2,1)S(1)}, bf16[16,32,128]{2,1,0:T(8,128)(2,1)S(1)}, bf16[16,32,128]{...) custom-call(s32[2]{0:T(128)S(1)} %pad_add_fusion.me_ref, f32[1,128]{1,0:T(1,128)S(1)} %add_add_fusion.2.refs_0_, ...), custom_call_target="tpu_custom_call" | custom-call | flops 1000000000 | bytes 6291456 | tf_op jit(solution)/shard_map/pallas_call | solution.py:454
  174.7 3.1 %shard_map.154 = (bf16[16,32,128]{2,1,0:T(8,128)(2,1)S(1)}, bf16[16,32,128]{2,1,0:T(8,128)(2,1)S(1)}, bf16[16,32,128]{2,1,0:T(8,128)(2,1)S(1)}, bf16[16,32,128]{2,1,0:T(8,128)(2,1)S(1)}) custom-call(s32[2]{0:T(128)S(1)} %pad_add_fusion.me_ref, f32[4096,128]{1,0:T(8,128)S(1)} %get-tuple-element.207.refs_0_.refs_2_.refs_3_.refs_6_, f32[4096,128]{1,0:T(8,128)S(1)} %bitcast.40, ...), custom_call_target="tpu_custom_call" | custom-call | flops 1000000000 | bytes 6291456 | tf_op jit(solution)/shard_map/pallas_call | solution.py:454
  184.9 1.7 collective-permute-done.58.refs_3_
  192.2 2.6 %inverse.10.refs_7_ = f32[4096,128]{1,0:T(8,128)S(1)} custom-call(s32[2]{0:T(128)S(1)} %pad_add_fusion.me_ref, bf16[16,32,128]{2,1,0:T(8,128)(2,1)S(1)} %get-tuple-element.221.refs_0_, bf16[16,32,128]{2,1,0:T(8,128)(2,1)S(1)} %collective-permute-done.65.refs_1_, bf16[16,32,128]{2,1,0:T(8,128)(2,1)S(1)} %collective-permute-done.66.refs_2_, ...), custom_call_target="tpu_custom_call" | custom-call | flops 1000000000 | bytes 4194304 | tf_op jit(solution)/shard_map/inverse/pallas_call | solution.py:578
  197.8 2.6 %inverse.11 = (bf16[8,256,128]{2,1,0:T(8,128)(2,1)S(1)}, bf16[8,256,128]{2,1,0:T(8,128)(2,1)S(1)}) custom-call(s32[2]{0:T(128)S(1)} %pad_add_fusion.me_ref, bf16[16,32,128]{2,1,0:T(8,128)(2,1)S(1)} %get-tuple-element.213.refs_0_, bf16[16,32,128]{2,1,0:T(8,128)(2,1)S(1)} %collective-permute-done.59.refs_1_, ...), custom_call_target="tpu_custom_call" | custom-call | flops 1000000000 | bytes 4194304 | tf_op jit(solution)/shard_map/inverse/pallas_call | solution.py:578
  203.7 5.5 %collective-permute-done.69 = bf16[4,256,128]{2,1,0:T(8,128)(2,1)S(1)} collective-permute-done((bf16[4,256,128]{2,1,0:T(8,128)(2,1)S(1)}, bf16[4,256,128]{2,1,0:T(8,128)(2,1)S(1)}, u32[]{:S(2)}, u32[]{:S(2)}) %collective-permute-start.69) | collective-permute-done | bytes 262176 | tf_op jit(solution)/shard_map/ppermute | solution.py:600
  212.4 2.4 collective-permute-done.73
  214.9 2.3 collective-permute-start.74
  217.2 2.3 collective-permute-start.71
  219.5 6.8 %collective-permute-done.74.got_ref = bf16[2,256,128]{2,1,0:T(8,128)(2,1)S(1)} collective-permute-done((bf16[2,256,128]{2,1,0:T(8,128)(2,1)S(1)}, bf16[2,256,128]{2,1,0:T(8,128)(2,1)S(1)}, u32[]{:S(2)}, u32[]{:S(2)}) %collective-permute-start.74) | collective-permute-done | bytes 131104 | tf_op jit(solution)/shard_map/ppermute | solution.py:600
  227.8 2.0 dots.5
  233.4 3.7 %collective-permute-done.75 = bf16[2,256,128]{2,1,0:T(8,128)(2,1)S(1)} collective-permute-done((bf16[2,256,128]{2,1,0:T(8,128)(2,1)S(1)}, bf16[2,256,128]{2,1,0:T(8,128)(2,1)S(1)}, u32[]{:S(2)}, u32[]{:S(2)}) %collective-permute-start.75) | collective-permute-done | bytes 131104 | tf_op jit(solution)/shard_map/ppermute | solution.py:600
  239.2 2.4 collective-permute-start.81
  242.6 3.7 %collective-permute-done.81 = f32[1,128]{1,0:T(1,128)S(1)} collective-permute-done((f32[1,128]{1,0:T(1,128)S(1)}, f32[1,128]{1,0:T(1,128)S(1)}, u32[]{:S(2)}, u32[]{:S(2)}) %collective-permute-start.81) | collective-permute-done | bytes 544 | tf_op jit(solution)/shard_map/ppermute | solution.py:600
  246.3 4.0 %shard_map.155 = (f32[4096,128]{1,0:T(8,128)}, f32[4096,128]{1,0:T(8,128)}) custom-call(s32[2]{0:T(128)S(1)} %pad_add_fusion.me_ref, f32[1,128]{1,0:T(1,128)S(1)} %add_add_fusion.refs_0_, f32[16,128]{1,0:T(8,128)S(1)} %get-tuple-element.241.refs_1_, bf16[4,256,128]{2,1,0:T(8,128)(2,1)S(1)} %pad_maximum_fusion.6.refs_2_, ...), custom_call_target="tpu_custom_call" | custom-call | flops 1000000000 | bytes 6291456 | tf_op jit(solution)/shard_map/pallas_call | solution.py:454
  (249 shorter events, 98.2 us)
Async XLA Ops:
  11.3 12.1 %collective-permute-start.6 = (bf16[16,32,128]{2,1,0:T(8,128)(2,1)}, bf16[16,32,128]{2,1,0:T(8,128)(2,1)S(1)}, u32[]{:S(2)}, u32[]{:S(2)}) collective-permute-start(bf16[16,32,128]{2,1,0:T(8,128)(2,1)} %get-tuple-element.136), channel_id=1, source_target_pairs={{0,1},{1,0},{2,3},{3,2},{4,5},{5,4},{6,7},{7,6},{8,9},{9,8},{10,11... | collective-permute-start | bytes 393224 | tf_op jit(solution)/shard_map/ppermute | solution.py:600
  11.8 11.7 %collective-permute-start.7 = (bf16[16,32,128]{2,1,0:T(8,128)(2,1)}, bf16[16,32,128]{2,1,0:T(8,128)(2,1)S(1)}, u32[]{:S(2)}, u32[]{:S(2)}) collective-permute-start(bf16[16,32,128]{2,1,0:T(8,128)(2,1)} %get-tuple-element.137), channel_id=1, source_target_pairs={{0,2},{1,3},{2,0},{3,1},{4,6},{5,7},{6,4},{7,5},{8,10},{9,11},{10,... | collective-permute-start | bytes 393224 | tf_op jit(solution)/shard_map/ppermute | solution.py:600
  14.3 9.2 %collective-permute-start.8 = (bf16[16,32,128]{2,1,0:T(8,128)(2,1)S(1)}, bf16[16,32,128]{2,1,0:T(8,128)(2,1)S(1)}, u32[]{:S(2)}, u32[]{:S(2)}) collective-permute-start(bf16[16,32,128]{2,1,0:T(8,128)(2,1)S(1)} %get-tuple-element.138), channel_id=1, source_target_pairs={{0,3},{1,2},{2,1},{3,0},{4,7},{5,6},{6,5},{7,4},{8,11},{9,10},{10,... | collective-permute-start | bytes 393224 | tf_op jit(solution)/shard_map/ppermute | solution.py:600
  17.2 10.1 %collective-permute-start = (bf16[16,32,128]{2,1,0:T(8,128)(2,1)S(1)}, bf16[16,32,128]{2,1,0:T(8,128)(2,1)S(1)}, u32[]{:S(2)}, u32[]{:S(2)}) collective-permute-start(bf16[16,32,128]{2,1,0:T(8,128)(2,1)S(1)} %get-tuple-element.128), channel_id=1, source_target_pairs={{0,1},{1,0},{2,3},{3,2},{4,5},{5,4},{6,7},{7,6},{8,9},{9,8},{10,11... | collective-permute-start | bytes 393224 | tf_op jit(solution)/shard_map/ppermute | solution.py:600
  17.4 9.9 %collective-permute-start.1 = (bf16[16,32,128]{2,1,0:T(8,128)(2,1)S(1)}, bf16[16,32,128]{2,1,0:T(8,128)(2,1)S(1)}, u32[]{:S(2)}, u32[]{:S(2)}) collective-permute-start(bf16[16,32,128]{2,1,0:T(8,128)(2,1)S(1)} %get-tuple-element.129), channel_id=1, source_target_pairs={{0,2},{1,3},{2,0},{3,1},{4,6},{5,7},{6,4},{7,5},{8,10},{9,11},{10,... | collective-permute-start | bytes 393224 | tf_op jit(solution)/shard_map/ppermute | solution.py:600
  25.4 7.1 %collective-permute-start.10 = (bf16[16,32,128]{2,1,0:T(8,128)(2,1)S(1)}, bf16[16,32,128]{2,1,0:T(8,128)(2,1)S(1)}, u32[]{:S(2)}, u32[]{:S(2)}) collective-permute-start(bf16[16,32,128]{2,1,0:T(8,128)(2,1)S(1)} %get-tuple-element.141), channel_id=1, source_target_pairs={{0,2},{1,3},{2,0},{3,1},{4,6},{5,7},{6,4},{7,5},{8,10},{9,11},{10,... | collective-permute-start | bytes 393224 | tf_op jit(solution)/shard_map/ppermute | solution.py:600
  27.3 7.4 %collective-permute-start.11 = (bf16[16,32,128]{2,1,0:T(8,128)(2,1)S(1)}, bf16[16,32,128]{2,1,0:T(8,128)(2,1)S(1)}, u32[]{:S(2)}, u32[]{:S(2)}) collective-permute-start(bf16[16,32,128]{2,1,0:T(8,128)(2,1)S(1)} %get-tuple-element.142), channel_id=1, source_target_pairs={{0,3},{1,2},{2,1},{3,0},{4,7},{5,6},{6,5},{7,4},{8,11},{9,10},{10,... | collective-permute-start | bytes 393224 | tf_op jit(solution)/shard_map/ppermute | solution.py:600
  30.4 7.1 %collective-permute-start.3 = (bf16[16,32,128]{2,1,0:T(8,128)(2,1)S(1)}, bf16[16,32,128]{2,1,0:T(8,128)(2,1)S(1)}, u32[]{:S(2)}, u32[]{:S(2)}) collective-permute-start(bf16[16,32,128]{2,1,0:T(8,128)(2,1)S(1)} %get-tuple-element.132), channel_id=1, source_target_pairs={{0,1},{1,0},{2,3},{3,2},{4,5},{5,4},{6,7},{7,6},{8,9},{9,8},{10,11... | collective-permute-start | bytes 393224 | tf_op jit(solution)/shard_map/ppermute | solution.py:600
  30.6 7.2 %collective-permute-start.4 = (bf16[16,32,128]{2,1,0:T(8,128)(2,1)S(1)}, bf16[16,32,128]{2,1,0:T(8,128)(2,1)S(1)}, u32[]{:S(2)}, u32[]{:S(2)}) collective-permute-start(bf16[16,32,128]{2,1,0:T(8,128)(2,1)S(1)} %get-tuple-element.133), channel_id=1, source_target_pairs={{0,2},{1,3},{2,0},{3,1},{4,6},{5,7},{6,4},{7,5},{8,10},{9,11},{10,... | collective-permute-start | bytes 393224 | tf_op jit(solution)/shard_map/ppermute | solution.py:600
  30.9 9.4 %collective-permute-start.5 = (bf16[16,32,128]{2,1,0:T(8,128)(2,1)S(1)}, bf16[16,32,128]{2,1,0:T(8,128)(2,1)S(1)}, u32[]{:S(2)}, u32[]{:S(2)}) collective-permute-start(bf16[16,32,128]{2,1,0:T(8,128)(2,1)S(1)} %get-tuple-element.134), channel_id=1, source_target_pairs={{0,3},{1,2},{2,1},{3,0},{4,7},{5,6},{6,5},{7,4},{8,11},{9,10},{10,... | collective-permute-start | bytes 393224 | tf_op jit(solution)/shard_map/ppermute | solution.py:600
  43.2 8.4 %collective-permute-start.13 = (bf16[4,256,128]{2,1,0:T(8,128)(2,1)S(1)}, bf16[4,256,128]{2,1,0:T(8,128)(2,1)S(1)}, u32[]{:S(2)}, u32[]{:S(2)}) collective-permute-start(bf16[4,256,128]{2,1,0:T(8,128)(2,1)S(1)} %slice.74), channel_id=1, source_target_pairs={{0,8},{4,12},{8,0},{12,4},{16,24},{20,28},{24,16},{28,20},{1,9},{5... | collective-permute-start | bytes 786440 | tf_op jit(solution)/shard_map/ppermute | solution.py:600
  44.8 8.0 %collective-permute-start.12 = (bf16[4,256,128]{2,1,0:T(8,128)(2,1)S(1)}, bf16[4,256,128]{2,1,0:T(8,128)(2,1)S(1)}, u32[]{:S(2)}, u32[]{:S(2)}) collective-permute-start(bf16[4,256,128]{2,1,0:T(8,128)(2,1)S(1)} %slice.73), channel_id=1, source_target_pairs={{0,4},{4,0},{8,12},{12,8},{16,20},{20,16},{24,28},{28,24},{1,5},{5... | collective-permute-start | bytes 786440 | tf_op jit(solution)/shard_map/ppermute | solution.py:600
  58.0 11.2 %collective-permute-start.18 = (bf16[2,256,128]{2,1,0:T(8,128)(2,1)S(1)}, bf16[2,256,128]{2,1,0:T(8,128)(2,1)S(1)}, u32[]{:S(2)}, u32[]{:S(2)}) collective-permute-start(bf16[2,256,128]{2,1,0:T(8,128)(2,1)S(1)} %add_convert_fusion.10.mine_ref), channel_id=1, source_target_pairs={{0,16},{4,20},{8,24},{12,28},{16,0},{20,4},{24,8},{28,12},{1,17},{... | collective-permute-start | bytes 393224 | tf_op jit(solution)/shard_map/ppermute | solution.py:600
  60.7 9.9 %collective-permute-start.15 = (bf16[2,256,128]{2,1,0:T(8,128)(2,1)S(1)}, bf16[2,256,128]{2,1,0:T(8,128)(2,1)S(1)}, u32[]{:S(2)}, u32[]{:S(2)}) collective-permute-start(bf16[2,256,128]{2,1,0:T(8,128)(2,1)S(1)} %add_convert_fusion.11.mine_ref), channel_id=1, source_target_pairs={{0,16},{4,20},{8,24},{12,28},{16,0},{20,4},{24,8},{28,12},{1,17},{... | collective-permute-start | bytes 393224 | tf_op jit(solution)/shard_map/ppermute | solution.py:600
  81.4 8.7 %collective-permute-start.26 = (bf16[4,256,128]{2,1,0:T(8,128)(2,1)S(1)}, bf16[4,256,128]{2,1,0:T(8,128)(2,1)S(1)}, u32[]{:S(2)}, u32[]{:S(2)}) collective-permute-start(bf16[4,256,128]{2,1,0:T(8,128)(2,1)S(1)} %pad_maximum_fusion.2.refs_1_.refs_0_), channel_id=1, source_target_pairs={{0,4},{4,0},{8,12},{12,8},{16,20},{20,16},{24,28},{28,24},{1,5},{5... | collective-permute-start | bytes 786440 | tf_op jit(solution)/shard_map/ppermute | solution.py:600
  82.0 8.1 %collective-permute-start.27 = (bf16[4,256,128]{2,1,0:T(8,128)(2,1)S(1)}, bf16[4,256,128]{2,1,0:T(8,128)(2,1)S(1)}, u32[]{:S(2)}, u32[]{:S(2)}) collective-permute-start(bf16[4,256,128]{2,1,0:T(8,128)(2,1)S(1)} %pad_maximum_fusion.3.refs_3_.refs_2_), channel_id=1, source_target_pairs={{0,8},{4,12},{8,0},{12,4},{16,24},{20,28},{24,16},{28,20},{1,9},{5... | collective-permute-start | bytes 786440 | tf_op jit(solution)/shard_map/ppermute | solution.py:600
  82.3 7.8 %collective-permute-start.25 = (f32[1,128]{1,0:T(1,128)S(1)}, f32[1,128]{1,0:T(1,128)S(1)}, u32[]{:S(2)}, u32[]{:S(2)}) collective-permute-start(f32[1,128]{1,0:T(1,128)S(1)} %add_add_fusion.5), channel_id=1, source_target_pairs={{0,12},{4,8},{8,4},{12,0},{16,28},{20,24},{24,20},{28,16},{1,13},{... | collective-permute-start | bytes 1544 | tf_op jit(solution)/shard_map/ppermute | solution.py:600
  96.4 7.1 %collective-permute-start.36 = (bf16[16,32,128]{2,1,0:T(8,128)(2,1)S(1)}, bf16[16,32,128]{2,1,0:T(8,128)(2,1)S(1)}, u32[]{:S(2)}, u32[]{:S(2)}) collective-permute-start(bf16[16,32,128]{2,1,0:T(8,128)(2,1)S(1)} %get-tuple-element.175), channel_id=1, source_target_pairs={{0,3},{1,2},{2,1},{3,0},{4,7},{5,6},{6,5},{7,4},{8,11},{9,10},{10,... | collective-permute-start | bytes 393224 | tf_op jit(solution)/shard_map/ppermute | solution.py:600
  101.5 7.6 %collective-permute-start.30 = (bf16[16,32,128]{2,1,0:T(8,128)(2,1)S(1)}, bf16[16,32,128]{2,1,0:T(8,128)(2,1)S(1)}, u32[]{:S(2)}, u32[]{:S(2)}) collective-permute-start(bf16[16,32,128]{2,1,0:T(8,128)(2,1)S(1)} %get-tuple-element.167), channel_id=1, source_target_pairs={{0,3},{1,2},{2,1},{3,0},{4,7},{5,6},{6,5},{7,4},{8,11},{9,10},{10,... | collective-permute-start | bytes 393224 | tf_op jit(solution)/shard_map/ppermute | solution.py:600
  104.8 7.6 %collective-permute-start.37 = (bf16[16,32,128]{2,1,0:T(8,128)(2,1)S(1)}, bf16[16,32,128]{2,1,0:T(8,128)(2,1)S(1)}, u32[]{:S(2)}, u32[]{:S(2)}) collective-permute-start(bf16[16,32,128]{2,1,0:T(8,128)(2,1)S(1)} %get-tuple-element.177), channel_id=1, source_target_pairs={{0,1},{1,0},{2,3},{3,2},{4,5},{5,4},{6,7},{7,6},{8,9},{9,8},{10,11... | collective-permute-start | bytes 393224 | tf_op jit(solution)/shard_map/ppermute | solution.py:600
  105.8 7.2 %collective-permute-start.38 = (bf16[16,32,128]{2,1,0:T(8,128)(2,1)S(1)}, bf16[16,32,128]{2,1,0:T(8,128)(2,1)S(1)}, u32[]{:S(2)}, u32[]{:S(2)}) collective-permute-start(bf16[16,32,128]{2,1,0:T(8,128)(2,1)S(1)} %get-tuple-element.178), channel_id=1, source_target_pairs={{0,2},{1,3},{2,0},{3,1},{4,6},{5,7},{6,4},{7,5},{8,10},{9,11},{10,... | collective-permute-start | bytes 393224 | tf_op jit(solution)/shard_map/ppermute | solution.py:600
  106.8 8.0 %collective-permute-start.39 = (bf16[16,32,128]{2,1,0:T(8,128)(2,1)S(1)}, bf16[16,32,128]{2,1,0:T(8,128)(2,1)S(1)}, u32[]{:S(2)}, u32[]{:S(2)}) collective-permute-start(bf16[16,32,128]{2,1,0:T(8,128)(2,1)S(1)} %get-tuple-element.179), channel_id=1, source_target_pairs={{0,3},{1,2},{2,1},{3,0},{4,7},{5,6},{6,5},{7,4},{8,11},{9,10},{10,... | collective-permute-start | bytes 393224 | tf_op jit(solution)/shard_map/ppermute | solution.py:600
  110.4 7.0 %collective-permute-start.31 = (bf16[16,32,128]{2,1,0:T(8,128)(2,1)S(1)}, bf16[16,32,128]{2,1,0:T(8,128)(2,1)S(1)}, u32[]{:S(2)}, u32[]{:S(2)}) collective-permute-start(bf16[16,32,128]{2,1,0:T(8,128)(2,1)S(1)} %get-tuple-element.169), channel_id=1, source_target_pairs={{0,1},{1,0},{2,3},{3,2},{4,5},{5,4},{6,7},{7,6},{8,9},{9,8},{10,11... | collective-permute-start | bytes 393224 | tf_op jit(solution)/shard_map/ppermute | solution.py:600
  111.4 7.2 %collective-permute-start.32 = (bf16[16,32,128]{2,1,0:T(8,128)(2,1)S(1)}, bf16[16,32,128]{2,1,0:T(8,128)(2,1)S(1)}, u32[]{:S(2)}, u32[]{:S(2)}) collective-permute-start(bf16[16,32,128]{2,1,0:T(8,128)(2,1)S(1)} %get-tuple-element.170), channel_id=1, source_target_pairs={{0,2},{1,3},{2,0},{3,1},{4,6},{5,7},{6,4},{7,5},{8,10},{9,11},{10,... | collective-permute-start | bytes 393224 | tf_op jit(solution)/shard_map/ppermute | solution.py:600
  112.4 8.0 %collective-permute-start.33 = (bf16[16,32,128]{2,1,0:T(8,128)(2,1)S(1)}, bf16[16,32,128]{2,1,0:T(8,128)(2,1)S(1)}, u32[]{:S(2)}, u32[]{:S(2)}) collective-permute-start(bf16[16,32,128]{2,1,0:T(8,128)(2,1)S(1)} %get-tuple-element.171), channel_id=1, source_target_pairs={{0,3},{1,2},{2,1},{3,0},{4,7},{5,6},{6,5},{7,4},{8,11},{9,10},{10,... | collective-permute-start | bytes 393224 | tf_op jit(solution)/shard_map/ppermute | solution.py:600
  123.2 8.6 %collective-permute-start.41 = (bf16[4,256,128]{2,1,0:T(8,128)(2,1)S(1)}, bf16[4,256,128]{2,1,0:T(8,128)(2,1)S(1)}, u32[]{:S(2)}, u32[]{:S(2)}) collective-permute-start(bf16[4,256,128]{2,1,0:T(8,128)(2,1)S(1)} %slice.82), channel_id=1, source_target_pairs={{0,8},{4,12},{8,0},{12,4},{16,24},{20,28},{24,16},{28,20},{1,9},{5... | collective-permute-start | bytes 786440 | tf_op jit(solution)/shard_map/ppermute | solution.py:600
  123.8 8.3 %collective-permute-start.40 = (bf16[4,256,128]{2,1,0:T(8,128)(2,1)S(1)}, bf16[4,256,128]{2,1,0:T(8,128)(2,1)S(1)}, u32[]{:S(2)}, u32[]{:S(2)}) collective-permute-start(bf16[4,256,128]{2,1,0:T(8,128)(2,1)S(1)} %slice.81), channel_id=1, source_target_pairs={{0,4},{4,0},{8,12},{12,8},{16,20},{20,16},{24,28},{28,24},{1,5},{5... | collective-permute-start | bytes 786440 | tf_op jit(solution)/shard_map/ppermute | solution.py:600
  133.0 7.2 %collective-permute-start.42 = (bf16[2,256,128]{2,1,0:T(8,128)(2,1)S(1)}, bf16[2,256,128]{2,1,0:T(8,128)(2,1)S(1)}, u32[]{:S(2)}, u32[]{:S(2)}) collective-permute-start(bf16[2,256,128]{2,1,0:T(8,128)(2,1)S(1)} %slice.101), channel_id=1, source_target_pairs={{0,8},{4,12},{8,0},{12,4},{16,24},{20,28},{24,16},{28,20},{1,9},{5... | collective-permute-start | bytes 393224 | tf_op jit(solution)/shard_map/ppermute | solution.py:600
  137.3 11.6 %collective-permute-start.46 = (bf16[2,256,128]{2,1,0:T(8,128)(2,1)S(1)}, bf16[2,256,128]{2,1,0:T(8,128)(2,1)S(1)}, u32[]{:S(2)}, u32[]{:S(2)}) collective-permute-start(bf16[2,256,128]{2,1,0:T(8,128)(2,1)S(1)} %add_convert_fusion.8.mine_ref), channel_id=1, source_target_pairs={{0,16},{4,20},{8,24},{12,28},{16,0},{20,4},{24,8},{28,12},{1,17},{... | collective-permute-start | bytes 393224 | tf_op jit(solution)/shard_map/ppermute | solution.py:600
  140.2 10.1 %collective-permute-start.43 = (bf16[2,256,128]{2,1,0:T(8,128)(2,1)S(1)}, bf16[2,256,128]{2,1,0:T(8,128)(2,1)S(1)}, u32[]{:S(2)}, u32[]{:S(2)}) collective-permute-start(bf16[2,256,128]{2,1,0:T(8,128)(2,1)S(1)} %add_convert_fusion.9.mine_ref), channel_id=1, source_target_pairs={{0,16},{4,20},{8,24},{12,28},{16,0},{20,4},{24,8},{28,12},{1,17},{... | collective-permute-start | bytes 393224 | tf_op jit(solution)/shard_map/ppermute | solution.py:600
  159.5 8.4 %collective-permute-start.54 = (bf16[4,256,128]{2,1,0:T(8,128)(2,1)S(1)}, bf16[4,256,128]{2,1,0:T(8,128)(2,1)S(1)}, u32[]{:S(2)}, u32[]{:S(2)}) collective-permute-start(bf16[4,256,128]{2,1,0:T(8,128)(2,1)S(1)} %pad_maximum_fusion.4.refs_2_.refs_0_), channel_id=1, source_target_pairs={{0,4},{4,0},{8,12},{12,8},{16,20},{20,16},{24,28},{28,24},{1,5},{5... | collective-permute-start | bytes 786440 | tf_op jit(solution)/shard_map/ppermute | solution.py:600
  160.7 7.1 %collective-permute-start.55 = (bf16[4,256,128]{2,1,0:T(8,128)(2,1)S(1)}, bf16[4,256,128]{2,1,0:T(8,128)(2,1)S(1)}, u32[]{:S(2)}, u32[]{:S(2)}) collective-permute-start(bf16[4,256,128]{2,1,0:T(8,128)(2,1)S(1)} %pad_maximum_fusion.5.refs_4_.refs_2_), channel_id=1, source_target_pairs={{0,8},{4,12},{8,0},{12,4},{16,24},{20,28},{24,16},{28,20},{1,9},{5... | collective-permute-start | bytes 786440 | tf_op jit(solution)/shard_map/ppermute | solution.py:600
  172.8 6.9 %collective-permute-start.63 = (bf16[16,32,128]{2,1,0:T(8,128)(2,1)S(1)}, bf16[16,32,128]{2,1,0:T(8,128)(2,1)S(1)}, u32[]{:S(2)}, u32[]{:S(2)}) collective-permute-start(bf16[16,32,128]{2,1,0:T(8,128)(2,1)S(1)} %get-tuple-element.219), channel_id=1, source_target_pairs={{0,2},{1,3},{2,0},{3,1},{4,6},{5,7},{6,4},{7,5},{8,10},{9,11},{10,... | collective-permute-start | bytes 393224 | tf_op jit(solution)/shard_map/ppermute | solution.py:600
  173.8 7.2 %collective-permute-start.64 = (bf16[16,32,128]{2,1,0:T(8,128)(2,1)S(1)}, bf16[16,32,128]{2,1,0:T(8,128)(2,1)S(1)}, u32[]{:S(2)}, u32[]{:S(2)}) collective-permute-start(bf16[16,32,128]{2,1,0:T(8,128)(2,1)S(1)} %get-tuple-element.220), channel_id=1, source_target_pairs={{0,3},{1,2},{2,1},{3,0},{4,7},{5,6},{6,5},{7,4},{8,11},{9,10},{10,... | collective-permute-start | bytes 393224 | tf_op jit(solution)/shard_map/ppermute | solution.py:600
  179.2 7.4 %collective-permute-start.58 = (bf16[16,32,128]{2,1,0:T(8,128)(2,1)S(1)}, bf16[16,32,128]{2,1,0:T(8,128)(2,1)S(1)}, u32[]{:S(2)}, u32[]{:S(2)}) collective-permute-start(bf16[16,32,128]{2,1,0:T(8,128)(2,1)S(1)} %get-tuple-element.212), channel_id=1, source_target_pairs={{0,3},{1,2},{2,1},{3,0},{4,7},{5,6},{6,5},{7,4},{8,11},{9,10},{10,... | collective-permute-start | bytes 393224 | tf_op jit(solution)/shard_map/ppermute | solution.py:600
  182.3 7.5 %collective-permute-start.65 = (bf16[16,32,128]{2,1,0:T(8,128)(2,1)S(1)}, bf16[16,32,128]{2,1,0:T(8,128)(2,1)S(1)}, u32[]{:S(2)}, u32[]{:S(2)}) collective-permute-start(bf16[16,32,128]{2,1,0:T(8,128)(2,1)S(1)} %get-tuple-element.222), channel_id=1, source_target_pairs={{0,1},{1,0},{2,3},{3,2},{4,5},{5,4},{6,7},{7,6},{8,9},{9,8},{10,11... | collective-permute-start | bytes 393224 | tf_op jit(solution)/shard_map/ppermute | solution.py:600
  183.3 7.2 %collective-permute-start.66 = (bf16[16,32,128]{2,1,0:T(8,128)(2,1)S(1)}, bf16[16,32,128]{2,1,0:T(8,128)(2,1)S(1)}, u32[]{:S(2)}, u32[]{:S(2)}) collective-permute-start(bf16[16,32,128]{2,1,0:T(8,128)(2,1)S(1)} %get-tuple-element.223), channel_id=1, source_target_pairs={{0,2},{1,3},{2,0},{3,1},{4,6},{5,7},{6,4},{7,5},{8,10},{9,11},{10,... | collective-permute-start | bytes 393224 | tf_op jit(solution)/shard_map/ppermute | solution.py:600
  184.2 8.0 %collective-permute-start.67 = (bf16[16,32,128]{2,1,0:T(8,128)(2,1)S(1)}, bf16[16,32,128]{2,1,0:T(8,128)(2,1)S(1)}, u32[]{:S(2)}, u32[]{:S(2)}) collective-permute-start(bf16[16,32,128]{2,1,0:T(8,128)(2,1)S(1)} %get-tuple-element.224), channel_id=1, source_target_pairs={{0,3},{1,2},{2,1},{3,0},{4,7},{5,6},{6,5},{7,4},{8,11},{9,10},{10,... | collective-permute-start | bytes 393224 | tf_op jit(solution)/shard_map/ppermute | solution.py:600
  187.9 6.9 %collective-permute-start.59 = (bf16[16,32,128]{2,1,0:T(8,128)(2,1)S(1)}, bf16[16,32,128]{2,1,0:T(8,128)(2,1)S(1)}, u32[]{:S(2)}, u32[]{:S(2)}) collective-permute-start(bf16[16,32,128]{2,1,0:T(8,128)(2,1)S(1)} %get-tuple-element.214), channel_id=1, source_target_pairs={{0,1},{1,0},{2,3},{3,2},{4,5},{5,4},{6,7},{7,6},{8,9},{9,8},{10,11... | collective-permute-start | bytes 393224 | tf_op jit(solution)/shard_map/ppermute | solution.py:600
  188.9 7.2 %collective-permute-start.60 = (bf16[16,32,128]{2,1,0:T(8,128)(2,1)S(1)}, bf16[16,32,128]{2,1,0:T(8,128)(2,1)S(1)}, u32[]{:S(2)}, u32[]{:S(2)}) collective-permute-start(bf16[16,32,128]{2,1,0:T(8,128)(2,1)S(1)} %get-tuple-element.215), channel_id=1, source_target_pairs={{0,2},{1,3},{2,0},{3,1},{4,6},{5,7},{6,4},{7,5},{8,10},{9,11},{10,... | collective-permute-start | bytes 393224 | tf_op jit(solution)/shard_map/ppermute | solution.py:600
  189.8 8.0 %collective-permute-start.61 = (bf16[16,32,128]{2,1,0:T(8,128)(2,1)S(1)}, bf16[16,32,128]{2,1,0:T(8,128)(2,1)S(1)}, u32[]{:S(2)}, u32[]{:S(2)}) collective-permute-start(bf16[16,32,128]{2,1,0:T(8,128)(2,1)S(1)} %get-tuple-element.216), channel_id=1, source_target_pairs={{0,3},{1,2},{2,1},{3,0},{4,7},{5,6},{6,5},{7,4},{8,11},{9,10},{10,... | collective-permute-start | bytes 393224 | tf_op jit(solution)/shard_map/ppermute | solution.py:600
  200.5 8.6 %collective-permute-start.69 = (bf16[4,256,128]{2,1,0:T(8,128)(2,1)S(1)}, bf16[4,256,128]{2,1,0:T(8,128)(2,1)S(1)}, u32[]{:S(2)}, u32[]{:S(2)}) collective-permute-start(bf16[4,256,128]{2,1,0:T(8,128)(2,1)S(1)} %slice.90), channel_id=1, source_target_pairs={{0,8},{4,12},{8,0},{12,4},{16,24},{20,28},{24,16},{28,20},{1,9},{5... | collective-permute-start | bytes 786440 | tf_op jit(solution)/shard_map/ppermute | solution.py:600
  201.4 8.3 %collective-permute-start.68 = (bf16[4,256,128]{2,1,0:T(8,128)(2,1)S(1)}, bf16[4,256,128]{2,1,0:T(8,128)(2,1)S(1)}, u32[]{:S(2)}, u32[]{:S(2)}) collective-permute-start(bf16[4,256,128]{2,1,0:T(8,128)(2,1)S(1)} %slice.89), channel_id=1, source_target_pairs={{0,4},{4,0},{8,12},{12,8},{16,20},{20,16},{24,28},{28,24},{1,5},{5... | collective-permute-start | bytes 786440 | tf_op jit(solution)/shard_map/ppermute | solution.py:600
  214.9 11.5 %collective-permute-start.74 = (bf16[2,256,128]{2,1,0:T(8,128)(2,1)S(1)}, bf16[2,256,128]{2,1,0:T(8,128)(2,1)S(1)}, u32[]{:S(2)}, u32[]{:S(2)}) collective-permute-start(bf16[2,256,128]{2,1,0:T(8,128)(2,1)S(1)} %add_convert_fusion.6.mine_ref), channel_id=1, source_target_pairs={{0,16},{4,20},{8,24},{12,28},{16,0},{20,4},{24,8},{28,12},{1,17},{... | collective-permute-start | bytes 393224 | tf_op jit(solution)/shard_map/ppermute | solution.py:600
  217.2 10.5 %collective-permute-start.71 = (bf16[2,256,128]{2,1,0:T(8,128)(2,1)S(1)}, bf16[2,256,128]{2,1,0:T(8,128)(2,1)S(1)}, u32[]{:S(2)}, u32[]{:S(2)}) collective-permute-start(bf16[2,256,128]{2,1,0:T(8,128)(2,1)S(1)} %add_convert_fusion.7.mine_ref), channel_id=1, source_target_pairs={{0,16},{4,20},{8,24},{12,28},{16,0},{20,4},{24,8},{28,12},{1,17},{... | collective-permute-start | bytes 393224 | tf_op jit(solution)/shard_map/ppermute | solution.py:600
  238.0 8.4 %collective-permute-start.82 = (bf16[4,256,128]{2,1,0:T(8,128)(2,1)S(1)}, bf16[4,256,128]{2,1,0:T(8,128)(2,1)S(1)}, u32[]{:S(2)}, u32[]{:S(2)}) collective-permute-start(bf16[4,256,128]{2,1,0:T(8,128)(2,1)S(1)} %pad_maximum_fusion.6.refs_2_), channel_id=1, source_target_pairs={{0,4},{4,0},{8,12},{12,8},{16,20},{20,16},{24,28},{28,24},{1,5},{5... | collective-permute-start | bytes 786440 | tf_op jit(solution)/shard_map/ppermute | solution.py:600
  238.9 7.5 %collective-permute-start.83 = (bf16[4,256,128]{2,1,0:T(8,128)(2,1)S(1)}, bf16[4,256,128]{2,1,0:T(8,128)(2,1)S(1)}, u32[]{:S(2)}, u32[]{:S(2)}) collective-permute-start(bf16[4,256,128]{2,1,0:T(8,128)(2,1)S(1)} %pad_maximum_fusion.7.refs_4_), channel_id=1, source_target_pairs={{0,8},{4,12},{8,0},{12,4},{16,24},{20,28},{24,16},{28,20},{1,9},{5... | collective-permute-start | bytes 786440 | tf_op jit(solution)/shard_map/ppermute | solution.py:600
  239.2 7.2 %collective-permute-start.81 = (f32[1,128]{1,0:T(1,128)S(1)}, f32[1,128]{1,0:T(1,128)S(1)}, u32[]{:S(2)}, u32[]{:S(2)}) collective-permute-start(f32[1,128]{1,0:T(1,128)S(1)} %add_add_fusion.1), channel_id=1, source_target_pairs={{0,12},{4,8},{8,4},{12,0},{16,28},{20,24},{24,20},{28,16},{1,13},{... | collective-permute-start | bytes 1544 | tf_op jit(solution)/shard_map/ppermute | solution.py:600
  (58 other events, 446.4 us)
